TPU v7x, 128 devices: a whole 4x4x4 slice. The times are simulated.
128 devices in a mesh: dp: 1, col: 16 (over z, y), row: 8 (over x, core).
Axes of the slice: x: 4, y: 4, z: 4, core: 2. Of those that a mesh axis runs over, the one named last changes fastest.
Arguments:
- hidden: bfloat16 [4096, 4096], P('dp', 'row')
- norm_gain: float32 [4096], P('row')
- w_head: bfloat16 [4096, 32000], P('row', 'col')
Outputs:
- output 1: float32 [4096, 32000], P('dp', ('col', 'row'))
- output 2: float32 [4096], P('dp')
All inputs are finite; a program needn't handle non-finite values.
Results may differ from a plain program's by a relative error of at most 0.001.
Values sent between devices are 32-bit elements.
A program may use at most 1 GiB of HBM per device.

v0:
```python
import jax
import jax.numpy as jnp
from jax import lax
from jax.sharding import PartitionSpec as P

EPS = 1e-5


def solution(mesh):
    row_count = mesh.shape["row"]

    def local_head(hidden, norm_gain, w_head):
        wide_hidden = hidden.astype(jnp.float32)
        local_sq = jnp.sum(wide_hidden * wide_hidden, axis=-1, keepdims=True)
        total_sq = lax.psum(local_sq, "row")
        mean_sq = total_sq / (hidden.shape[1] * row_count)
        normed = (wide_hidden * lax.rsqrt(mean_sq + EPS) * norm_gain).astype(jnp.bfloat16)
        share_logits = jnp.dot(normed, w_head, preferred_element_type=jnp.float32)
        logits = lax.psum_scatter(share_logits, "row", scatter_dimension=1, tiled=True)
        local_max = jnp.max(logits, axis=-1, keepdims=True)
        global_max = lax.pmax(local_max, ("col", "row"))
        local_mass = jnp.sum(jnp.exp(logits - global_max), axis=-1, keepdims=True)
        total_mass = lax.psum(local_mass, ("col", "row"))
        log_norm = global_max + jnp.log(total_mass)
        return logits - log_norm, log_norm[:, 0]

    return jax.shard_map(
        local_head,
        mesh=mesh,
        in_specs=(P("dp", "row"), P("row"), P("row", "col")),
        out_specs=(P("dp", ("col", "row")), P("dp")),
        check_vma=False,
    )
```

profile of v0, /device:TPU:0, one launch (start us, length us, event | category | flops | bytes accessed | tf_op | source)
XLA Modules:
  0.0 544.2 jit_solution(15616682773690143669)
XLA Ops:
  7.2 0.0 copy-start
  7.2 0.0 copy-start.3
  7.2 0.0 all-reduce.3.cloned.1.call-start
  7.2 3.2 fusion
  10.5 25.8 %psum.14 = f32[4096,1]{0,1:T(1,128)S(1)} all-reduce(f32[4096,1]{0,1:T(1,128)S(1)} %bitcast.13), channel_id=1, replica_groups=mesh['dp'=1,'col'=16,'row'=8] {'row'}, use_global_device_ids=true, to_apply=%region_1.0 | all-reduce | flops 4096 | bytes 32768 | tf_op jit(solution)/shard_map/psum | solution.py:15
  36.3 0.0 copy-done
  36.3 0.0 copy-done.3
  36.3 17.5 %fusion.3 = f32[4096,2000]{1,0:T(8,128)} fusion(bf16[512,2000]{0,1:T(8,128)(2,1)S(1)} %copy-done, bf16[4096,512]{1,0:T(8,128)(2,1)} %param.3, f32[512]{0:T(512)S(1)} %copy-done.3, f32[4096]{0:T(1024)S(1)} %bitcast.16), kind=kOutput, calls=%fused_computation.5 | convolution fusion | flops 8396996608 | bytes 39028736 | tf_op jit(solution)/shard_map/dot_general | solution.py:18
  53.8 0.0 copy-start.4
  53.8 0.0 all-reduce.3.cloned.1.call-update
  53.8 0.6 copy-done.4
  54.4 0.6 dynamic-slice
  55.7 338.2 %all-reduce.3.cloned.1.call-done = f32[4096,2000]{1,0:T(8,128)} async-done(((f32[4096,2000]{1,0:T(8,128)}), f32[4096,2000]{1,0:T(8,128)}) %all-reduce.3.cloned.1.call-update) | async-done | bytes 32768016
  393.8 4.5 dynamic-slice_reduce_fusion
  398.4 65.4 %pmax.7 = f32[4096,1]{0,1:T(1,128)S(1)} all-reduce(f32[4096,1]{0,1:T(1,128)S(1)} %bitcast.14), channel_id=1, replica_groups=mesh['dp'=1,'col'=16,'row'=8] {'col','row'}, use_global_device_ids=true, to_apply=%region_4.0 | all-reduce | flops 4096 | bytes 32768 | tf_op jit(solution)/shard_map/pmax | solution.py:21
  463.8 4.5 exponential_reduce_fusion
  468.3 63.8 %psum.15 = f32[4096,1]{0,1:T(1,128)S(1)} all-reduce(f32[4096,1]{0,1:T(1,128)S(1)} %bitcast.15), channel_id=1, replica_groups=mesh['dp'=1,'col'=16,'row'=8] {'col','row'}, use_global_device_ids=true, to_apply=%region_6.0 | all-reduce | flops 4096 | bytes 32768 | tf_op jit(solution)/shard_map/psum | solution.py:23
  532.2 0.0 copy-start.2
  532.2 0.0 copy-start.1
  532.2 5.2 dynamic-slice_subtract_fusion
  537.4 0.0 copy-done.2
  537.4 0.0 copy-done.1
  (2 shorter events, 0.1 us)
Async XLA Ops:
  7.2 29.1 %copy-start = (bf16[512,2000]{0,1:T(8,128)(2,1)S(1)}, bf16[512,2000]{0,1:T(8,128)(2,1)}, u32[]{:S(2)}) copy-start(bf16[512,2000]{0,1:T(8,128)(2,1)} %param.5) | copy-start | bytes 6144004
  7.2 29.1 %copy-start.3 = (f32[512]{0:T(512)S(1)}, f32[512]{0:T(512)}, u32[]{:S(2)}) copy-start(f32[512]{0:T(512)} %param.4) | copy-start | bytes 6148
  7.2 386.7 %all-reduce.3.cloned.1.call-start = ((), (), s32[]{:S(2)}) async-start(), calls=%async_computation | async-start | bytes 67108864
  53.8 0.7 copy-start.4
  532.2 5.2 copy-start.2
  532.2 5.2 copy-start.1
Sparse Core Ops, SparseCore 0:
  53.9 339.8 all-reduce.2
where the time goes:
time: 545 us; the launch traced here: 544 us
  waiting for transfers between devices  338 us (62%)
  blocking collectives  155 us (28%)
  other arithmetic  17.5 us (3%)
  matrix products  17.5 us (3%)
  between operations  14.8 us (3%)
    unnamed x2, waiting for transfers between devices  338 us
    pmax x1, blocking collectives, local_head(): global_max = lax.pmax(local_max, ('col', 'row'))  65.4 us
    psum x1, blocking collectives, local_head(): total_mass = lax.psum(local_mass, ('col', 'row'))  63.8 us
    psum x1, blocking collectives, local_head(): total_sq = lax.psum(local_sq, 'row')  25.8 us
    dot_general x1, matrix products, local_head(): share_logits = jnp.dot(normed, w_head, preferred_element_type=jnp.float32)  17.5 us
  transfers between devices with their start and end apart: 1, of which 1 were waited for; matrix products, arithmetic and copies ran while one was open for 0% of the time, Pallas kernels for 0%

commit v1 on v0

v1 whole, which is shorter than its diff:
```python
import jax
import jax.numpy as jnp
from jax import lax
from jax.sharding import PartitionSpec as P

EPS = 1e-5


def solution(mesh):
    row_count = mesh.shape["row"]

    def local_head(hidden, norm_gain, w_head):
        wide_hidden = hidden.astype(jnp.float32)
        local_sq = jnp.sum(wide_hidden * wide_hidden, axis=-1)
        total_sq = lax.psum(local_sq, "row")[:, None]
        mean_sq = total_sq / (hidden.shape[1] * row_count)
        normed = (wide_hidden * lax.rsqrt(mean_sq + EPS) * norm_gain).astype(jnp.bfloat16)
        words = w_head.shape[1] // row_count
        pad = -words % 128
        blocks = jnp.pad(w_head.reshape(w_head.shape[0], row_count, words), ((0, 0), (0, 0), (0, pad)))
        share = jnp.einsum("sk,kbw->bsw", normed, blocks, preferred_element_type=jnp.float32)
        logits = lax.psum_scatter(share, "row", scatter_dimension=0, tiled=False)[:, :words]
        local_max = jnp.max(logits, axis=-1)
        global_max = lax.pmax(local_max, ("col", "row"))
        local_mass = jnp.sum(jnp.exp(logits - global_max[:, None]), axis=-1)
        total_mass = lax.psum(local_mass, ("col", "row"))
        log_norm = global_max + jnp.log(total_mass)
        return logits - log_norm[:, None], log_norm

    return jax.shard_map(
        local_head,
        mesh=mesh,
        in_specs=(P("dp", "row"), P("row"), P("row", "col")),
        out_specs=(P("dp", ("col", "row")), P("dp")),
        check_vma=False,
    )
```

time: 545 us -> 378 us (0.69)
  waiting for transfers between devices: 338 us -> 171 us
  local copies, waits for them, and re-layouts: 1.24 us -> 7.42 us
    unnamed x2 -> x1, waiting for transfers between devices: 338 us -> 0.02 us
    reduce_scatter x0 -> x1, waiting for transfers between devices: none -> 170 us  [local_head(): lax.psum_scatter(share, 'row', scatter_dimension=0, tiled=False)[:, :words]]
where the time goes in v1:
time: 378 us; the launch traced here: 377 us
  waiting for transfers between devices  171 us (45%)
  blocking collectives  155 us (41%)
  matrix products  17.5 us (5%)
  between operations  14.1 us (4%)
  other arithmetic  13 us (3%)
  local copies, waits for them, and re-layouts  7.42 us (2%)
    reduce_scatter x1, waiting for transfers between devices, local_head(): lax.psum_scatter(share, 'row', scatter_dimension=0, tiled=False)[:, :words]  170 us
    pmax x1, blocking collectives, local_head(): global_max = lax.pmax(local_max, ('col', 'row'))  65.2 us
    psum x1, blocking collectives, local_head(): total_mass = lax.psum(local_mass, ('col', 'row'))  63.8 us
    psum x1, blocking collectives, local_head(): total_sq = lax.psum(local_sq, 'row')[:, None]  25.8 us
    dot_general x1, matrix products, local_head(): jnp.einsum('sk,kbw->bsw', normed, blocks, preferred_element_type=jnp.floa...  17.5 us
  transfers between devices with their start and end apart: 1, of which 1 were waited for; matrix products, arithmetic and copies ran while one was open for 0% of the time, Pallas kernels for 0%

profile of v1, /device:TPU:0, one launch (start us, length us, event | category | flops | bytes accessed | tf_op | source)
XLA Modules:
  0.0 377.3 jit_solution(6856787835194648220)
XLA Ops:
  7.2 0.0 copy-start.1
  7.2 0.0 reduce-scatter.2.cloned.1.call-start
  7.2 3.1 fusion
  10.3 25.8 %psum.14 = f32[4096]{0:T(1024)S(1)} all-reduce(f32[4096]{0:T(1024)S(1)} %fusion), channel_id=1, replica_groups=mesh['dp'=1,'col'=16,'row'=8] {'row'}, use_global_device_ids=true, to_apply=%region_1.0 | all-reduce | flops 4096 | bytes 32768 | tf_op jit(solution)/shard_map/psum | solution.py:15
  36.1 1.8 reshape.14
  37.9 0.0 copy-done.1
  37.9 17.5 %convolution_bitcast_fusion = f32[8,4096,256]{1,2,0:T(8,128)} fusion(bf16[4096,512]{1,0:T(8,128)(2,1)} %param.3, f32[512]{0:T(512)S(1)} %copy-done.1, f32[4096]{0:T(1024)S(1)} %add_rsqrt_fusion, bf16[512,8,250]{0,2,1:T(8,128)(2,1)S(1)} %reshape.14), kind=kOutput, calls=%fused_computation | convolution fusion | flops 8598323200 | bytes 39815168 | tf_op jit(solution)/shard_map/sk,kbw->bsw/dot_general | solution.py:21
  55.5 0.0 reduce-scatter.2.cloned.1.call-update
  55.5 170.5 %reduce-scatter.2.cloned.1.call-done = f32[1,4096,256]{1,2,0:T(8,128)} async-done(((f32[8,4096,256]{1,2,0:T(8,128)}), f32[1,4096,256]{1,2,0:T(8,128)}) %reduce-scatter.2.cloned.1.call-update) | async-done | bytes 4194320 | tf_op jit(solution)/shard_map/reduce_scatter | solution.py:22
  226.0 2.4 slice_reduce_fusion
  228.4 65.2 %pmax.7 = f32[4096]{0:T(1024)S(1)} all-reduce(f32[4096]{0:T(1024)S(1)} %slice_reduce_fusion), channel_id=1, replica_groups=mesh['dp'=1,'col'=16,'row'=8] {'col','row'}, use_global_device_ids=true, to_apply=%region_4.5 | all-reduce | flops 4096 | bytes 32768 | tf_op jit(solution)/shard_map/pmax | solution.py:24
  293.5 2.8 exponential_reduce_fusion
  296.3 63.8 %psum.15 = f32[4096]{0:T(1024)S(1)} all-reduce(f32[4096]{0:T(1024)S(1)} %exponential_reduce_fusion), channel_id=1, replica_groups=mesh['dp'=1,'col'=16,'row'=8] {'col','row'}, use_global_device_ids=true, to_apply=%region_6.7 | all-reduce | flops 4096 | bytes 32768 | tf_op jit(solution)/shard_map/psum | solution.py:26
  360.2 0.0 copy-start
  360.2 4.7 %slice_subtract_fusion = f32[4096,250]{0,1:T(8,128)} fusion(f32[4096,256]{0,1:T(8,128)} %bitcast.10, f32[4096]{0:T(1024)S(1)} %log_add_fusion), kind=kLoop, calls=%fused_computation.10 | loop fusion | flops 1024000 | bytes 8208384 | tf_op jit(solution)/shard_map/sub | solution.py:28
  364.9 0.0 copy-done
  364.9 5.6 %copy.6 = f32[4096,250]{1,0:T(8,128)} copy(f32[4096,250]{0,1:T(8,128)} %slice_subtract_fusion) | data formatting | bytes 8192000
  (2 shorter events, 0.0 us)
Async XLA Ops:
  7.2 30.7 %copy-start.1 = (f32[512]{0:T(512)S(1)}, f32[512]{0:T(512)}, u32[]{:S(2)}) copy-start(f32[512]{0:T(512)} %param.4) | copy-start | bytes 6148
  7.2 218.8 %reduce-scatter.2.cloned.1.call-start = ((), (), s32[]{:S(2)}) async-start(), calls=%async_computation.1 | async-start | bytes 37748736 | tf_op jit(solution)/shard_map/reduce_scatter | solution.py:22
  360.2 4.7 %copy-start = (f32[4096]{0:T(1024)}, f32[4096]{0:T(1024)S(1)}, u32[]{:S(2)}) copy-start(f32[4096]{0:T(1024)S(1)} %log_add_fusion) | copy-start | bytes 49156
Sparse Core Ops, SparseCore 0:
  55.6 170.3 reduce-scatter.1

commit v2 on v0

v2 whole, which is shorter than its diff:
```python
import functools

import jax
import jax.numpy as jnp
from jax import lax
from jax.experimental import pallas as pl
from jax.experimental.pallas import tpu as pltpu
from jax.sharding import PartitionSpec as P

EPS = 1e-5
MESH = pl.DeviceIdType.MESH
F32 = jnp.float32
BF16 = jnp.bfloat16
LOW = -3.0e38

SEQ, FEAT, WORDS, PAD = 4096, 512, 250, 256
HALF = SEQ // 2
BLOCK, PIECE = 128, 32


def kernel(h_hbm, g_ref, w_hbm, z_hbm, lse_ref,
           h, w, wst, wl, wbf, xst, xl, xbf, zs, zp, zr, ssq, rinv, st1, st2, st3,
           in_sem, ssq_send, ssq_recv, wp_send, wp_recv, wb_send, wb_recv, wr_send, wr_recv,
           xp_send, xp_recv, xb_send, xf_send, x_recv, z_send, z_recv, zp_send, zp_recv,
           out_sem, st_send, st1_recv, st2_recv, st3_recv):
    col, row = lax.axis_index("col"), lax.axis_index("row")
    z, y = lax.div(col, 4), lax.rem(col, 4)
    x, c = lax.div(row, 2), lax.rem(row, 2)
    mate = 1 - c
    near = x + 1 - 2 * lax.rem(x, 2)
    far = 3 - x

    def at_row(r):
        return (0, col, r)

    def at_col(yy, zz):
        return (0, zz * 4 + yy, row)

    partner = at_row(x * 2 + mate)
    near_same = at_row(near * 2 + c)

    def remote(src, dst, send, recv, dev):
        return pltpu.make_async_remote_copy(
            src_ref=src, dst_ref=dst, send_sem=send, recv_sem=recv, device_id=dev, device_id_type=MESH)

    def drain_send(ref, sem):
        remote(ref, ref, sem, sem, partner).wait_send()

    def drain_recv(ref, sem):
        remote(ref, ref, sem, sem, partner).wait_recv()

    for k in range(4):
        rows = pl.ds(k * 1024, 1024)
        pltpu.make_async_copy(h_hbm.at[rows, :], h.at[rows, :], in_sem.at[k]).start()
    w_in = pltpu.make_async_copy(w_hbm, w, in_sem.at[4])
    w_in.start()

    barrier = pltpu.get_barrier_semaphore()
    peers = [at_row(lax.rem(row + d, 8)) for d in range(1, 8)]
    peers += [at_col(lax.rem(y + d, 4), z) for d in range(1, 4)]
    peers += [at_col(y, lax.rem(z + d, 4)) for d in range(1, 4)]
    for dev in peers:
        pl.semaphore_signal(barrier, inc=1, device_id=dev, device_id_type=MESH)

    w_in.wait()

    def prep(t, _):
        rows = pl.ds(pl.multiple_of(t * 64, 64), 64)
        wide = w[rows, :].astype(F32)
        for b in range(8):
            part = wide[:, b * WORDS:(b + 1) * WORDS]
            wst[b, rows, :] = jnp.concatenate([part, jnp.zeros((64, PAD - WORDS), F32)], axis=1)
        return 0

    lax.fori_loop(0, FEAT // 64, prep, 0)
    pl.semaphore_wait(barrier, len(peers))

    def kind_block(chip, n):
        return ((3 - chip) * 2 + n) if n < 2 else (chip * 2 + n - 2)

    def send_near(n, k0, size):
        rows = pl.ds(k0, size)
        remote(wst.at[kind_block(near, n), rows, :], wl.at[1, n, rows, :], wb_send, wb_recv.at[n], near_same).start()

    send_near(0, 0, 256)

    for k in range(4):
        rows = pl.ds(k * 1024, 1024)
        pltpu.make_async_copy(h_hbm.at[rows, :], h.at[rows, :], in_sem.at[k]).wait()

        def squares(t, _, k=k):
            b = k * 8 + t
            hb = h[pl.ds(pl.multiple_of(b * BLOCK, BLOCK), BLOCK), :].astype(F32)
            sq = hb * hb
            part = (sq[:, 0:128] + sq[:, 128:256]) + (sq[:, 256:384] + sq[:, 384:512])
            ssq[row, pl.ds(b, 1), :] = jnp.sum(part.T, axis=0, keepdims=True)
            return 0

        lax.fori_loop(0, 8, squares, 0)
    for d in range(1, 8):
        remote(ssq.at[row], ssq.at[row], ssq_send, ssq_recv.at[row], at_row(lax.rem(row + d, 8))).start()

    send_near(0, 256, 256)
    for n in range(4):
        remote(wst.at[kind_block(x, n)], wl.at[0, n], wp_send, wp_recv.at[n], partner).start()

    for d in range(1, 8):
        r = lax.rem(row + d, 8)
        drain_recv(ssq.at[r], ssq_recv.at[r])
    total = ssq[0]
    for r in range(1, 8):
        total = total + ssq[r]
    rinv[...] = lax.rsqrt(total / (FEAT * 8) + EPS)

    def flow(f):
        t, s = lax.div(f, 2), 1 - 2 * lax.rem(f, 2)
        return y * (1 - t) + z * t, z * (1 - t) + y * t, s

    def first(f, i):
        c1, _, s = flow(f)
        return lax.rem(c1 - s * i + 4, 4)

    def second(f, j):
        _, c2, s = flow(f)
        return lax.rem(c2 - s * j + 4, 4)

    def norm_block(nb):
        rows = pl.ds(pl.multiple_of(nb * BLOCK, BLOCK), BLOCK)
        scale = jnp.broadcast_to(rinv[pl.ds(nb, 1), :], (BLOCK, BLOCK)).T
        for q in range(4):
            lanes = slice(q * 128, (q + 1) * 128)
            value = h[rows, lanes].astype(F32) * scale * g_ref[:, lanes]
            xst[rows, lanes] = value.astype(BF16).astype(F32)

    def send_mate(n):
        i, f = lax.div(n, 4), lax.rem(n, 4)
        blk = f * 4 + first(f, i)
        src = pl.ds(pl.multiple_of(mate * HALF + blk * BLOCK, BLOCK), BLOCK)
        dst = pl.ds(pl.multiple_of(blk * BLOCK, BLOCK), BLOCK)
        remote(xst.at[src, :], xl.at[0, dst, :], xp_send, xp_recv.at[blk], partner).start()

    def norm_step(n, _):
        i, f = lax.div(n, 4), lax.rem(n, 4)
        blk = f * 4 + first(f, i)
        norm_block(blk)
        norm_block(16 + blk)
        send_mate(n)

        @pl.when(i == 0)
        def _():
            piece = blk * BLOCK + second(f, 0) * PIECE
            dst = pl.ds(pl.multiple_of(piece, PIECE), PIECE)
            for core in range(2):
                src = pl.ds(pl.multiple_of(core * HALF + piece, PIECE), PIECE)
                slot = 1 + (core + c) - 2 * core * c
                remote(xst.at[src, :], xl.at[slot, dst, :], xb_send, x_recv.at[f, 0],
                       at_row(near * 2 + core)).start()
        return 0

    lax.fori_loop(0, 4, norm_step, 0)
    for n in range(1, 4):
        send_near(n, 0, FEAT)
    lax.fori_loop(4, 16, norm_step, 0)

    def relay_weights(n):
        drain_recv(wl.at[1, n], wb_recv.at[n])
        remote(wl.at[1, n], wl.at[2, n], wr_send, wr_recv.at[n], partner).start()

    def take_weights(n):
        drain_recv(wl.at[0, n], wp_recv.at[n])
        drain_recv(wl.at[2, n], wr_recv.at[n])
        wbf[n, 0:512, :] = wst[kind_block(x, n)].astype(BF16)
        for k in range(3):
            wbf[n, (k + 1) * 512:(k + 2) * 512, :] = wl[k, n].astype(BF16)

    ups = (at_col(lax.rem(y + 1, 4), z), at_col(lax.rem(y + 3, 4), z),
           at_col(y, lax.rem(z + 1, 4)), at_col(y, lax.rem(z + 3, 4)))
    along_first = (ups[0], ups[1], ups[2], ups[3])
    along_second = (ups[2], ups[3], ups[0], ups[1])

    def serve(i, j):
        for f in range(4):
            base = f * 512 + first(f, i) * BLOCK + second(f, j) * PIECE
            ref = xl.at[pl.ds(1, 2), pl.ds(pl.multiple_of(base, PIECE), PIECE), :]
            step = i * 4 + j
            drain_recv(ref, x_recv.at[f, step])

            @pl.when(j < 3)
            def _():
                remote(ref, ref, xf_send.at[f], x_recv.at[f, step + 1], along_second[f]).start()

            @pl.when((j == 0) & (i < 3))
            def _():
                remote(ref, ref, xf_send.at[f], x_recv.at[f, step + 4], along_first[f]).start()

    relay_weights(0)
    lax.fori_loop(0, 4, lambda j, _: (serve(0, j), 0)[1], 0)
    take_weights(0)

    def rows_of(n):
        i, f = lax.div(n, 4), lax.rem(n, 4)
        blk = f * 4 + first(f, i)
        return blk, pl.multiple_of(blk * BLOCK, BLOCK)

    def gather_block(blk, base):
        rows = pl.ds(base, BLOCK)
        drain_recv(xl.at[0, rows, :], xp_recv.at[blk])
        xbf[rows, 0:512] = xst[pl.ds(pl.multiple_of(c * HALF + base, BLOCK), BLOCK), :].astype(BF16)
        for k in range(3):
            xbf[rows, (k + 1) * 512:(k + 2) * 512] = xl[k, rows, :].astype(BF16)

    def far_block(n, blk, base):
        rows = pl.ds(base, BLOCK)
        zs[n, rows, :] = jnp.dot(xbf[rows, :], wbf[n], preferred_element_type=F32)
        remote(zs.at[n, rows, :], zr.at[c, rows, :], z_send.at[n], z_recv.at[c, blk], at_row(far * 2 + n)).start()

    def step_a(n, _):
        serve(1, n)
        blk, base = rows_of(n)
        gather_block(blk, base)
        far_block(0, blk, base)
        return 0

    lax.fori_loop(0, 4, step_a, 0)
    relay_weights(1)
    take_weights(1)

    def step_ab(n, _):
        @pl.when(n < 12)
        def _():
            serve(lax.div(n, 4) + 1, lax.rem(n, 4))

        blk, base = rows_of(n)
        gather_block(blk, base)
        far_block(0, blk, base)
        far_block(1, blk, base)
        return 0

    lax.fori_loop(4, 8, step_ab, 0)
    relay_weights(2)
    lax.fori_loop(8, 12, step_ab, 0)
    relay_weights(3)
    lax.fori_loop(12, 16, step_ab, 0)

    def step_b(n, _):
        blk, base = rows_of(n)
        far_block(1, blk, base)
        return 0

    lax.fori_loop(0, 4, step_b, 0)
    take_weights(2)
    take_weights(3)

    def step_own(n, _):
        blk, base = rows_of(n)
        rows = pl.ds(base, BLOCK)
        xl[0, rows, 256:512] = jnp.dot(xbf[rows, :], wbf[2 + mate], preferred_element_type=F32)
        remote(xl.at[0, rows, pl.ds(256, 256)], zp.at[rows, :], zp_send, zp_recv.at[blk], partner).start()
        xl[0, rows, 0:256] = jnp.dot(xbf[rows, :], wbf[2 + c], preferred_element_type=F32)
        return 0

    lax.fori_loop(0, 16, step_own, 0)

    def finish(half, blk, base, mine):
        rows = pl.ds(base, BLOCK)
        drain_recv(zr.at[half, rows, :], z_recv.at[half, blk])
        value = zr[half, rows, :] + mine
        zr[half, rows, :] = value
        pltpu.make_async_copy(
            zr.at[half, rows, :],
            z_hbm.at[pl.ds(pl.multiple_of(half * HALF + base, BLOCK), BLOCK), :], out_sem.at[half]).start()
        lane = lax.broadcasted_iota(jnp.int32, (BLOCK, 128), 1)
        left, right = value[:, 0:128], jnp.where(lane < WORDS - 128, value[:, 128:256], LOW)
        top = jnp.max(jnp.maximum(left, right).T, axis=0, keepdims=True)
        shift = jnp.broadcast_to(top, (BLOCK, BLOCK)).T
        mass = jnp.exp(left - shift) + jnp.exp(right - shift)
        nb = half * 16 + blk
        st1[row, 0, pl.ds(nb, 1), :] = top
        st1[row, 1, pl.ds(nb, 1), :] = jnp.sum(mass.T, axis=0, keepdims=True)

    def step_out(n, _):
        blk, base = rows_of(n)
        rows = pl.ds(base, BLOCK)
        finish(c, blk, base, xl[0, rows, 0:256])
        drain_recv(zp.at[rows, :], zp_recv.at[blk])
        finish(mate, blk, base, zp[rows, :])
        return 0

    lax.fori_loop(0, 16, step_out, 0)

    def combine(st, count):
        top = st[0, 0]
        for k in range(1, count):
            top = jnp.maximum(top, st[k, 0])
        mass = st[0, 1] * jnp.exp(st[0, 0] - top)
        for k in range(1, count):
            mass = mass + st[k, 1] * jnp.exp(st[k, 0] - top)
        return top, mass

    def exchange(st, me, count, send, recv, dev):
        for d in range(1, count):
            remote(st.at[me], st.at[me], send, recv.at[me], dev(lax.rem(me + d, count))).start()
        for d in range(1, count):
            other = lax.rem(me + d, count)
            drain_recv(st.at[other], recv.at[other])

    exchange(st1, row, 8, st_send.at[0], st1_recv, at_row)
    top, mass = combine(st1, 8)
    st2[z, 0], st2[z, 1] = top, mass
    exchange(st2, z, 4, st_send.at[1], st2_recv, lambda k: at_col(y, k))
    top, mass = combine(st2, 4)
    st3[y, 0], st3[y, 1] = top, mass
    exchange(st3, y, 4, st_send.at[2], st3_recv, lambda k: at_col(k, z))
    top, mass = combine(st3, 4)
    lse_ref[...] = top + jnp.log(mass)

    drain_send(ssq.at[pl.ds(0, 7)], ssq_send)
    drain_send(wl.at[0], wp_send)
    drain_send(wl.at[0], wb_send)
    drain_send(wl.at[0], wr_send)
    drain_send(xl.at[0], xp_send)
    drain_send(xl.at[0, pl.ds(0, 256), :], xb_send)
    for f in range(4):
        drain_send(xl.at[pl.ds(1, 2), pl.ds(0, 15 * PIECE), :], xf_send.at[f])
    for n in range(2):
        drain_send(zs.at[n], z_send.at[n])
    drain_send(zp, zp_send)
    drain_send(st1.at[pl.ds(0, 7)], st_send.at[0])
    drain_send(st2.at[pl.ds(0, 3)], st_send.at[1])
    drain_send(st3.at[pl.ds(0, 3)], st_send.at[2])
    for half in range(2):
        pltpu.make_async_copy(zr.at[half], z_hbm.at[pl.ds(half * HALF, HALF), :], out_sem.at[half]).wait()


def solution(mesh):
    dma = pltpu.SemaphoreType.DMA

    def local_head(hidden, norm_gain, w_head):
        logits, log_norm = pl.pallas_call(
            kernel,
            out_shape=(jax.ShapeDtypeStruct((SEQ, PAD), F32), jax.ShapeDtypeStruct((32, 128), F32)),
            in_specs=[pl.BlockSpec(memory_space=pl.ANY), pl.BlockSpec(memory_space=pltpu.VMEM),
                      pl.BlockSpec(memory_space=pl.ANY)],
            out_specs=(pl.BlockSpec(memory_space=pl.ANY), pl.BlockSpec(memory_space=pltpu.VMEM)),
            scratch_shapes=[
                pltpu.VMEM((SEQ, FEAT), BF16),
                pltpu.VMEM((FEAT, 8 * WORDS), BF16),
                pltpu.VMEM((8, FEAT, PAD), F32),
                pltpu.VMEM((3, 4, FEAT, PAD), F32),
                pltpu.VMEM((4, 4 * FEAT, PAD), BF16),
                pltpu.VMEM((SEQ, FEAT), F32),
                pltpu.VMEM((3, HALF, FEAT), F32),
                pltpu.VMEM((HALF, 4 * FEAT), BF16),
                pltpu.VMEM((2, HALF, PAD), F32),
                pltpu.VMEM((HALF, PAD), F32),
                pltpu.VMEM((2, HALF, PAD), F32),
                pltpu.VMEM((8, 32, 128), F32),
                pltpu.VMEM((32, 128), F32),
                pltpu.VMEM((8, 2, 32, 128), F32),
                pltpu.VMEM((4, 2, 32, 128), F32),
                pltpu.VMEM((4, 2, 32, 128), F32),
                dma((5,)),
                dma, dma((8,)),
                dma, dma((4,)),
                dma, dma((4,)),
                dma, dma((4,)),
                dma, dma((16,)),
                dma, dma((4,)), dma((4, 16)),
                dma((2,)), dma((2, 16)),
                dma, dma((16,)),
                dma((2,)),
                dma((3,)), dma((8,)), dma((4,)), dma((4,)),
            ],
            compiler_params=pltpu.CompilerParams(
                collective_id=0, has_side_effects=True, vmem_limit_bytes=67_043_328),
        )(hidden, norm_gain.reshape(1, FEAT), w_head)
        log_norm = log_norm.reshape(SEQ)
        return logits[:, :WORDS] - log_norm[:, None], log_norm

    return jax.shard_map(
        local_head,
        mesh=mesh,
        in_specs=(P("dp", "row"), P("row"), P("row", "col")),
        out_specs=(P("dp", ("col", "row")), P("dp")),
        check_vma=False,
    )
```

time: 545 us -> 182 us (0.33)
  waiting for transfers between devices: 338 us -> 0 us
  Pallas kernels: 0 us -> 173 us
  blocking collectives: 155 us -> 0 us
  matrix products: 17.5 us -> 0 us
  between operations: 14.8 us -> 0.65 us
  other arithmetic: 17.5 us -> 4.16 us
    unnamed x2 -> x0, waiting for transfers between devices: 338 us -> none
    pallas_call x0 -> x1, Pallas kernels: none -> 173 us  [local_head(): pl.pallas_call(kernel, out_shape=(jax.ShapeDtypeStruct((SEQ, PAD), F32),...]
    psum x2 -> x0, blocking collectives: 89.6 us -> none  [the longest x1 63.8 us: local_head(): total_mass = lax.psum(local_mass, ('col', 'row'))]
    pmax x1 -> x0, blocking collectives: 65.4 us -> none  [local_head(): global_max = lax.pmax(local_max, ('col', 'row'))]
    dot_general x1 -> x0, matrix products: 17.5 us -> none  [local_head(): share_logits = jnp.dot(normed, w_head, preferred_element_type=jnp.float32)]
    reduce_sum x2 -> x0, other arithmetic: 7.74 us -> none  [the longest x1 4.52 us: local_head(): local_mass = jnp.sum(jnp.exp(logits - global_max), axis=-1, keepdims=True)]
  transfers between devices with their start and end apart: 1 -> 0, of which waited for: 1 -> 0; matrix products, arithmetic and copies ran while one was open for 0% -> 0% of each run, Pallas kernels for 0% -> 0%
where the time goes in v2:
time: 182 us
  Pallas kernels  173 us (95%)
  local copies, waits for them, and re-layouts  4.49 us (2%)
  other arithmetic  4.16 us (2%)
    pallas_call x1, Pallas kernels, local_head(): pl.pallas_call(kernel, out_shape=(jax.ShapeDtypeStruct((SEQ, PAD), F32),...  173 us
    unnamed x4, local copies, waits for them, and re-layouts  4.49 us
    sub x1, other arithmetic, local_head(): return (logits[:, :WORDS] - log_norm[:, None], log_norm)  4.16 us

profile of v2, /device:TPU:0, one launch (start us, length us, event | category | flops | bytes accessed | tf_op | source)
XLA Modules:
  0.0 182.1 jit_solution(9577008166344391975)
XLA Ops:
  0.6 3.9 %copy.5.w_hbm = bf16[512,2000]{1,0:T(8,128)(2,1)} copy(bf16[512,2000]{0,1:T(8,128)(2,1)} %param.5) | data formatting | bytes 4096000 | tf_op args[2]
  4.5 172.8 %shard_map.50 = (f32[4096,256]{1,0:T(8,128)}, f32[32,128]{1,0:T(8,128)}) custom-call(bf16[4096,512]{1,0:T(8,128)(2,1)} %h_hbm.1, f32[1,512]{1,0:T(1,128)} %bitcast.4, bf16[512,2000]{1,0:T(8,128)(2,1)} %copy.5.w_hbm), custom_call_target="tpu_custom_call" | custom-call | tf_op jit(solution)/shard_map/pallas_call | solution.py:339
  177.3 0.0 copy-start
  177.3 4.2 %slice_subtract_fusion = f32[4096,250]{1,0:T(8,128)} fusion(f32[4096,256]{1,0:T(8,128)} %get-tuple-element.4, f32[4096]{0:T(1024)} %bitcast.2), kind=kLoop, calls=%fused_computation | loop fusion | flops 1024000 | bytes 8208384 | tf_op jit(solution)/shard_map/sub | solution.py:378
  181.5 0.0 copy-done
  181.5 0.6 copy.7
Async XLA Ops:
  177.3 4.2 %copy-start = (f32[32,128]{1,0:T(8,128)S(1)}, f32[32,128]{1,0:T(8,128)}, u32[]{:S(2)}) copy-start(f32[32,128]{1,0:T(8,128)} %get-tuple-element.5) | copy-start | bytes 49156

commit v3 on v0

v3 whole, which is shorter than its diff:
```python
import functools

import jax
import jax.numpy as jnp
from jax import lax
from jax.experimental import pallas as pl
from jax.experimental.pallas import tpu as pltpu
from jax.sharding import PartitionSpec as P

EPS = 1e-5
MESH = pl.DeviceIdType.MESH
F32 = jnp.float32
BF16 = jnp.bfloat16
LOW = -3.0e38

SEQ, FEAT, WORDS, PAD = 4096, 512, 250, 256
HALF = SEQ // 2
BLOCK, PIECE = 128, 32
AHEAD = 7


def kernel(h_hbm, g_ref, w_hbm, z_hbm, lse_ref,
           h, hp16, hp, w, wst, wl, wbf, xst, xl, xbf, zs, zp, zr, gl, ssq, rcol, st1, st2, st3,
           in_sem, ssq_send, ssq_recv, g_send, g_recv, wp_send, wp_recv, wb_send, wb_recv, wr_send, wr_recv,
           xp_send, xp_recv, xb_send, xf_send, x_recv, z_send, z_recv, zp_send, zp_recv,
           out_sem, st_send, st1_recv, st2_recv, st3_recv):
    col, row = lax.axis_index("col"), lax.axis_index("row")
    z, y = lax.div(col, 4), lax.rem(col, 4)
    x, c = lax.div(row, 2), lax.rem(row, 2)
    mate = 1 - c
    near = x + 1 - 2 * lax.rem(x, 2)
    far = 3 - x

    def at_row(r):
        return (0, col, r)

    def at_col(yy, zz):
        return (0, zz * 4 + yy, row)

    partner = at_row(x * 2 + mate)
    near_same = at_row(near * 2 + c)
    near_other = at_row(near * 2 + mate)

    def remote(src, dst, send, recv, dev):
        return pltpu.make_async_remote_copy(
            src_ref=src, dst_ref=dst, send_sem=send, recv_sem=recv, device_id=dev, device_id_type=MESH)

    def drain_send(ref, sem):
        remote(ref, ref, sem, sem, partner).wait_send()

    def drain_recv(ref, sem):
        remote(ref, ref, sem, sem, partner).wait_recv()

    firsts, seconds = (y, y, z, z), (z, z, y, y)
    signs = (1, -1, 1, -1)

    def first(f, i):
        return lax.rem(firsts[f] - signs[f] * i + 4, 4)

    def second(f, j):
        return lax.rem(seconds[f] - signs[f] * j + 4, 4)

    def piece_base(f, i, j):
        return f * 512 + first(f, i) * BLOCK + second(f, j) * PIECE

    def piece_rows(f, i, j, offset=0):
        return pl.ds(pl.multiple_of(offset + piece_base(f, i, j), PIECE), PIECE)

    own_pieces = [(f, core) for f in range(4) for core in range(2)]

    def load_piece(f, core):
        return pltpu.make_async_copy(
            h_hbm.at[piece_rows(f, 0, 0, core * HALF), :], hp16.at[f * 2 + core], in_sem.at[5 + f * 2 + core])

    def load_h(k):
        rows = pl.ds(k * 1024, 1024)
        return pltpu.make_async_copy(h_hbm.at[rows, :], h.at[rows, :], in_sem.at[k])

    for f, core in own_pieces:
        load_piece(f, core).start()
    w_in = pltpu.make_async_copy(w_hbm, w, in_sem.at[4])
    w_in.start()
    for k in range(4):
        load_h(k).start()

    barrier = pltpu.get_barrier_semaphore()
    peers = [at_row(lax.rem(row + d, 8)) for d in range(1, 8)]
    peers += [at_col(lax.rem(y + d, 4), z) for d in range(1, 4)]
    peers += [at_col(y, lax.rem(z + d, 4)) for d in range(1, 4)]
    for dev in peers:
        pl.semaphore_signal(barrier, inc=1, device_id=dev, device_id_type=MESH)

    for f, core in own_pieces:
        load_piece(f, core).wait()
        hp[f * 2 + core] = hp16[f * 2 + core].astype(F32)
    with jax.named_scope("bar"):
        pl.semaphore_wait(barrier, len(peers))

    for f, core in own_pieces:
        slot = 1 + (core + c) - 2 * core * c
        remote(hp.at[f * 2 + core], xl.at[slot, piece_rows(f, 0, 0), :], xb_send, x_recv.at[f, 0],
               at_row(near * 2 + core)).start()
    for slot, dev in enumerate((partner, near_same, near_other)):
        remote(g_ref, gl.at[slot], g_send, g_recv.at[slot], dev).start()

    w_in.wait()

    def prep(b, rows):
        start = rows // 16 * 16
        for q in range(4):
            lanes = slice(q * 128, (q + 1) * 128)
            wide = w[start:min(start + 272, 8 * WORDS), lanes].astype(F32)
            part = wide[rows - start:rows - start + WORDS, :]
            wst[b, :, lanes] = jnp.concatenate([part, jnp.zeros((PAD - WORDS, 128), F32)], axis=0)

    with jax.named_scope("prep"):
        for b in range(8):
            prep(b, b * WORDS)

    def kind_block(chip, n):
        return ((3 - chip) * 2 + n) if n < 2 else (chip * 2 + n - 2)

    def send_near(n):
        remote(wst.at[kind_block(near, n)], wl.at[1, n], wb_send, wb_recv.at[n], near_same).start()

    send_near(0)
    for n in range(4):
        remote(wst.at[kind_block(x, n)], wl.at[0, n], wp_send, wp_recv.at[n], partner).start()

    for k in range(4):
        load_h(k).wait()

        def squares(t, _, k=k):
            b = k * 8 + t
            hb = h[pl.ds(pl.multiple_of(b * BLOCK, BLOCK), BLOCK), :].astype(F32)
            sq = hb * hb
            part = (sq[:, 0:128] + sq[:, 128:256]) + (sq[:, 256:384] + sq[:, 384:512])
            ssq[row, pl.ds(b, 1), :] = jnp.sum(part.T, axis=0, keepdims=True)
            return 0

        with jax.named_scope("squares"):
            lax.fori_loop(0, 8, squares, 0)
    for d in range(1, 8):
        remote(ssq.at[row], ssq.at[row], ssq_send, ssq_recv.at[row], at_row(lax.rem(row + d, 8))).start()
    for n in range(1, 4):
        send_near(n)

    for f in range(4):
        rows = pl.ds(f * 512, 512)
        xst[rows, :] = h[pl.ds(pl.multiple_of(mate * HALF + f * 512, 512), 512), :].astype(F32)
        remote(xst.at[rows, :], xl.at[0, rows, :], xp_send, xp_recv.at[f], partner).start()

    def relay_weights(n):
        with jax.named_scope("wrelay"):
            drain_recv(wl.at[1, n], wb_recv.at[n])
        remote(wl.at[1, n], wl.at[2, n], wr_send, wr_recv.at[n], partner).start()

    def take_weights(n):
        with jax.named_scope("wtake"):
            drain_recv(wl.at[0, n], wp_recv.at[n])
            drain_recv(wl.at[2, n], wr_recv.at[n])
        wbf[n, :, 0:512] = wst[kind_block(x, n)].astype(BF16)
        for k in range(3):
            wbf[n, :, (k + 1) * 512:(k + 2) * 512] = wl[k, n].astype(BF16)

    ups = (at_col(lax.rem(y + 1, 4), z), at_col(lax.rem(y + 3, 4), z),
           at_col(y, lax.rem(z + 1, 4)), at_col(y, lax.rem(z + 3, 4)))
    along_first = (ups[0], ups[1], ups[2], ups[3])
    along_second = (ups[2], ups[3], ups[0], ups[1])

    def serve(i, j):
        with jax.named_scope("serve"):
            for f in range(4):
                ref = xl.at[pl.ds(1, 2), piece_rows(f, i, j), :]
                step = i * 4 + j
                drain_recv(ref, x_recv.at[f, step])
                if j == 0 and i < 3:
                    remote(ref, ref, xf_send.at[f], x_recv.at[f, step + 4], along_first[f]).start()
                if j < 3:
                    remote(ref, ref, xf_send.at[f], x_recv.at[f, step + 1], along_second[f]).start()

    def scales():
        with jax.named_scope("wssq"):
            for d in range(1, 8):
                r = lax.rem(row + d, 8)
                drain_recv(ssq.at[r], ssq_recv.at[r])
            for slot in range(3):
                drain_recv(gl.at[slot], g_recv.at[slot])
        mine = pl.ds(pl.multiple_of(c * 16, 16), 16)
        total = ssq[0, mine, :]
        for r in range(1, 8):
            total = total + ssq[r, mine, :]
        inv = lax.rsqrt(total / (FEAT * 8) + EPS)
        for b in range(16):
            rcol[b * BLOCK:(b + 1) * BLOCK, :] = jnp.broadcast_to(inv[b:b + 1, :], (BLOCK, BLOCK)).T

    def normalise(f, i, j):
        rows = piece_rows(f, i, j)
        scale = rcol[rows, :]
        for k in range(4):
            for q in range(4):
                lanes = slice(q * 128, (q + 1) * 128)
                if k == 0:
                    raw, gain = h[piece_rows(f, i, j, c * HALF), lanes].astype(F32), g_ref[:, lanes]
                else:
                    raw, gain = xl[k - 1, rows, lanes], gl[k - 1, :, lanes]
                xbf[rows, k * 512 + q * 128:k * 512 + (q + 1) * 128] = (raw * scale * gain).astype(BF16)

    def share(left, n):
        return lax.dot_general(left, wbf[n], (((1,), (1,)), ((), ())), preferred_element_type=F32)

    def far_group(i, j):
        with jax.named_scope("group"):
            for f in range(4):
                normalise(f, i, j)
            left = jnp.concatenate([xbf[piece_rows(f, i, j), :] for f in range(4)], axis=0)
            value = share(left, 0)
            for f in range(4):
                rows = piece_rows(f, i, j)
                zs[0, rows, :] = value[f * PIECE:(f + 1) * PIECE, :]
                remote(zs.at[0, rows, :], zr.at[c, rows, :], z_send.at[0], z_recv.at[c, f * 4 + first(f, i)],
                       at_row(far * 2)).start()

    order = sorted(((i, j) for i in range(4) for j in range(4)), key=lambda t: (t[0] + t[1], -t[0]))
    ahead = AHEAD
    for i, j in order[:ahead - 2]:
        serve(i, j)
    scales()
    serve(*order[ahead - 2])
    relay_weights(0)
    serve(*order[ahead - 1])
    for f in range(4):
        drain_recv(xl.at[0, pl.ds(f * 512, 512), :], xp_recv.at[f])
    with jax.named_scope("take"):
        take_weights(0)
    for k, (i, j) in enumerate(order):
        far_group(i, j)
        if k > 0 and k + ahead - 1 < 16:
            serve(*order[k + ahead - 1])
        if k == 6:
            relay_weights(1)
        if k == 10:
            relay_weights(2)
    with jax.named_scope("take"):
        take_weights(1)

    def block_rows(blk):
        return pl.ds(pl.multiple_of(blk * BLOCK, BLOCK), BLOCK)

    def step_far(blk, _):
        with jax.named_scope("far"):
            rows = block_rows(blk)
            zs[1, rows, :] = share(xbf[rows, :], 1)
            remote(zs.at[1, rows, :], zr.at[c, rows, :], z_send.at[1], z_recv.at[c, blk], at_row(far * 2 + 1)).start()
        return 0

    lax.fori_loop(0, 16, step_far, 0)
    relay_weights(3)
    take_weights(2)
    take_weights(3)

    def step_own(blk, _):
        with jax.named_scope("own"):
            rows = block_rows(blk)
            xl[0, rows, 256:512] = share(xbf[rows, :], 2 + mate)
            remote(xl.at[0, rows, pl.ds(256, 256)], zp.at[rows, :], zp_send, zp_recv.at[blk], partner).start()
            xl[0, rows, 0:256] = share(xbf[rows, :], 2 + c)
        return 0

    lax.fori_loop(0, 16, step_own, 0)

    def finish(p, half, q, mine):
        blk = p * 4 + q
        rows = block_rows(blk)
        with jax.named_scope("wz"):
            drain_recv(zr.at[half, rows, :], z_recv.at[half, blk])
        value = zr[half, rows, :] + mine
        zr[half, rows, :] = value
        pltpu.make_async_copy(
            zr.at[half, rows, :],
            z_hbm.at[pl.ds(pl.multiple_of(half * HALF + blk * BLOCK, BLOCK), BLOCK), :], out_sem.at[half]).start()
        lane = lax.broadcasted_iota(jnp.int32, (BLOCK, 128), 1)
        left, right = value[:, 0:128], jnp.where(lane < WORDS - 128, value[:, 128:256], LOW)
        top = jnp.max(jnp.maximum(left, right).T, axis=0, keepdims=True)
        shift = jnp.broadcast_to(top, (BLOCK, BLOCK)).T
        mass = jnp.exp(left - shift) + jnp.exp(right - shift)
        st1[p, row, 0, pl.ds(half * 4 + q, 1), :] = top
        st1[p, row, 1, pl.ds(half * 4 + q, 1), :] = jnp.sum(mass.T, axis=0, keepdims=True)

    def combine(st, p, count):
        top = st[p, 0, 0]
        for k in range(1, count):
            top = jnp.maximum(top, st[p, k, 0])
        mass = st[p, 0, 1] * jnp.exp(st[p, 0, 0] - top)
        for k in range(1, count):
            mass = mass + st[p, k, 1] * jnp.exp(st[p, k, 0] - top)
        return top, mass

    def exchange(st, p, me, count, send, recv, dev):
        with jax.named_scope("exch"):
            for d in range(1, count):
                remote(st.at[p, me], st.at[p, me], send, recv.at[p, me], dev(lax.rem(me + d, count))).start()
            for d in range(1, count):
                other = lax.rem(me + d, count)
                drain_recv(st.at[p, other], recv.at[p, other])

    for p in range(4):
        def step_out(q, _, p=p):
            rows = block_rows(p * 4 + q)
            finish(p, c, q, xl[0, rows, 0:256])
            drain_recv(zp.at[rows, :], zp_recv.at[p * 4 + q])
            finish(p, mate, q, zp[rows, :])
            return 0

        with jax.named_scope("finish"):
            lax.fori_loop(0, 4, step_out, 0)
        exchange(st1, p, row, 8, st_send.at[0], st1_recv, at_row)
        top, mass = combine(st1, p, 8)
        st2[p, z, 0], st2[p, z, 1] = top, mass
        exchange(st2, p, z, 4, st_send.at[1], st2_recv, lambda k: at_col(y, k))
        top, mass = combine(st2, p, 4)
        st3[p, y, 0], st3[p, y, 1] = top, mass
        exchange(st3, p, y, 4, st_send.at[2], st3_recv, lambda k: at_col(k, z))
        top, mass = combine(st3, p, 4)
        lse = top + jnp.log(mass)
        for half in range(2):
            lse_ref[half * 16 + p * 4:half * 16 + p * 4 + 4, :] = lse[half * 4:half * 4 + 4, :]

    drain_send(ssq.at[pl.ds(0, 7)], ssq_send)
    drain_send(gl, g_send)
    drain_send(wl.at[0], wp_send)
    drain_send(wl.at[0], wb_send)
    drain_send(wl.at[0], wr_send)
    drain_send(xl.at[0], xp_send)
    drain_send(xl.at[0, pl.ds(0, 256), :], xb_send)
    for f in range(4):
        drain_send(xl.at[pl.ds(1, 2), pl.ds(0, 15 * PIECE), :], xf_send.at[f])
    for n in range(2):
        drain_send(zs.at[n], z_send.at[n])
    drain_send(zp, zp_send)
    drain_send(st1.at[:, pl.ds(0, 7)], st_send.at[0])
    drain_send(st2.at[:, pl.ds(0, 3)], st_send.at[1])
    drain_send(st3.at[:, pl.ds(0, 3)], st_send.at[2])
    for half in range(2):
        pltpu.make_async_copy(zr.at[half], z_hbm.at[pl.ds(half * HALF, HALF), :], out_sem.at[half]).wait()


def solution(mesh):
    dma = pltpu.SemaphoreType.DMA

    def local_head(hidden, norm_gain, w_head):
        logits, log_norm = pl.pallas_call(
            kernel,
            out_shape=(jax.ShapeDtypeStruct((SEQ, PAD), F32), jax.ShapeDtypeStruct((32, 128), F32)),
            in_specs=[pl.BlockSpec(memory_space=pl.ANY), pl.BlockSpec(memory_space=pltpu.VMEM),
                      pl.BlockSpec(memory_space=pl.ANY)],
            out_specs=(pl.BlockSpec(memory_space=pl.ANY), pl.BlockSpec(memory_space=pltpu.VMEM)),
            scratch_shapes=[
                pltpu.VMEM((SEQ, FEAT), BF16),
                pltpu.VMEM((8, PIECE, FEAT), BF16),
                pltpu.VMEM((8, PIECE, FEAT), F32),
                pltpu.VMEM((8 * WORDS, FEAT), BF16),
                pltpu.VMEM((8, PAD, FEAT), F32),
                pltpu.VMEM((3, 4, PAD, FEAT), F32),
                pltpu.VMEM((4, PAD, 4 * FEAT), BF16),
                pltpu.VMEM((HALF, FEAT), F32),
                pltpu.VMEM((3, HALF, FEAT), F32),
                pltpu.VMEM((HALF, 4 * FEAT), BF16),
                pltpu.VMEM((2, HALF, PAD), F32),
                pltpu.VMEM((HALF, PAD), F32),
                pltpu.VMEM((2, HALF, PAD), F32),
                pltpu.VMEM((3, 1, FEAT), F32),
                pltpu.VMEM((8, 32, 128), F32),
                pltpu.VMEM((HALF, 128), F32),
                pltpu.VMEM((4, 8, 2, 8, 128), F32),
                pltpu.VMEM((4, 4, 2, 8, 128), F32),
                pltpu.VMEM((4, 4, 2, 8, 128), F32),
                dma((13,)),
                dma, dma((8,)),
                dma, dma((3,)),
                dma, dma((4,)),
                dma, dma((4,)),
                dma, dma((4,)),
                dma, dma((4,)),
                dma, dma((4,)), dma((4, 16)),
                dma((2,)), dma((2, 16)),
                dma, dma((16,)),
                dma((2,)),
                dma((3,)), dma((4, 8)), dma((4, 4)), dma((4, 4)),
            ],
            compiler_params=pltpu.CompilerParams(
                collective_id=0, has_side_effects=True, vmem_limit_bytes=67_043_328),
        )(hidden, norm_gain.reshape(1, FEAT), w_head.T)
        log_norm = log_norm.reshape(SEQ)
        return logits[:, :WORDS] - log_norm[:, None], log_norm

    return jax.shard_map(
        local_head,
        mesh=mesh,
        in_specs=(P("dp", "row"), P("row"), P("row", "col")),
        out_specs=(P("dp", ("col", "row")), P("dp")),
        check_vma=False,
    )
```

time: 545 us -> 186 us (0.34)
  waiting for transfers between devices: 338 us -> 0 us
  Pallas kernels: 0 us -> 181 us
  blocking collectives: 155 us -> 0 us
  matrix products: 17.5 us -> 0 us
  between operations: 14.8 us -> 0.65 us
  other arithmetic: 17.5 us -> 4.16 us
    unnamed x2 -> x0, waiting for transfers between devices: 338 us -> none
    pallas_call x0 -> x1, Pallas kernels: none -> 181 us  [local_head(): pl.pallas_call(kernel, out_shape=(jax.ShapeDtypeStruct((SEQ, PAD), F32),...]
    psum x2 -> x0, blocking collectives: 89.6 us -> none  [the longest x1 63.8 us: local_head(): total_mass = lax.psum(local_mass, ('col', 'row'))]
    pmax x1 -> x0, blocking collectives: 65.4 us -> none  [local_head(): global_max = lax.pmax(local_max, ('col', 'row'))]
    dot_general x1 -> x0, matrix products: 17.5 us -> none  [local_head(): share_logits = jnp.dot(normed, w_head, preferred_element_type=jnp.float32)]
    reduce_sum x2 -> x0, other arithmetic: 7.74 us -> none  [the longest x1 4.52 us: local_head(): local_mass = jnp.sum(jnp.exp(logits - global_max), axis=-1, keepdims=True)]
  transfers between devices with their start and end apart: 1 -> 0, of which waited for: 1 -> 0; matrix products, arithmetic and copies ran while one was open for 0% -> 0% of each run, Pallas kernels for 0% -> 0%
where the time goes in v3:
time: 186 us
  Pallas kernels  181 us (97%)
  other arithmetic  4.16 us (2%)
    pallas_call x1, Pallas kernels, local_head(): pl.pallas_call(kernel, out_shape=(jax.ShapeDtypeStruct((SEQ, PAD), F32),...  181 us
    sub x1, other arithmetic, local_head(): return (logits[:, :WORDS] - log_norm[:, None], log_norm)  4.16 us

profile of v3, /device:TPU:0, one launch (start us, length us, event | category | flops | bytes accessed | tf_op | source)
XLA Modules:
  0.0 186.2 jit_solution(16505965011323751976)
XLA Ops:
  0.6 180.8 %shard_map.50 = (f32[4096,256]{1,0:T(8,128)}, f32[32,128]{1,0:T(8,128)}) custom-call(bf16[4096,512]{1,0:T(8,128)(2,1)} %h_hbm.1, f32[1,512]{1,0:T(1,128)} %bitcast.6, bf16[2000,512]{1,0:T(8,128)(2,1)} %bitcast.3), custom_call_target="tpu_custom_call" | custom-call | tf_op jit(solution)/shard_map/pallas_call | solution.py:352
  181.5 0.0 copy-start
  181.5 4.2 %slice_subtract_fusion = f32[4096,250]{1,0:T(8,128)} fusion(f32[4096,256]{1,0:T(8,128)} %get-tuple-element.4, f32[4096]{0:T(1024)} %bitcast.4), kind=kLoop, calls=%fused_computation | loop fusion | flops 1024000 | bytes 8208384 | tf_op jit(solution)/shard_map/sub | solution.py:395
  185.6 0.0 copy-done
  185.6 0.6 copy.6
Async XLA Ops:
  181.5 4.2 %copy-start = (f32[32,128]{1,0:T(8,128)S(1)}, f32[32,128]{1,0:T(8,128)}, u32[]{:S(2)}) copy-start(f32[32,128]{1,0:T(8,128)} %get-tuple-element.5) | copy-start | bytes 49156

commit v4 on v3

--- a/solution.py
+++ b/solution.py
@@ -16,11 +16,10 @@
 SEQ, FEAT, WORDS, PAD = 4096, 512, 250, 256
 HALF = SEQ // 2
 BLOCK, PIECE = 128, 32
-AHEAD = 7
 
 
 def kernel(h_hbm, g_ref, w_hbm, z_hbm, lse_ref,
-           h, hp16, hp, w, wst, wl, wbf, xst, xl, xbf, zs, zp, zr, gl, ssq, rcol, st1, st2, st3,
+           h, hp16, hp, w, wst, wl, wbf, xst, xl, xbf, zs, zp, zr, gl, ssq, rcol, st, st1, st2, st3,
            in_sem, ssq_send, ssq_recv, g_send, g_recv, wp_send, wp_recv, wb_send, wb_recv, wr_send, wr_recv,
            xp_send, xp_recv, xb_send, xf_send, x_recv, z_send, z_recv, zp_send, zp_recv,
            out_sem, st_send, st1_recv, st2_recv, st3_recv):
@@ -120,10 +119,13 @@
     def kind_block(chip, n):
         return ((3 - chip) * 2 + n) if n < 2 else (chip * 2 + n - 2)
 
-    def send_near(n):
-        remote(wst.at[kind_block(near, n)], wl.at[1, n], wb_send, wb_recv.at[n], near_same).start()
-
-    send_near(0)
+    parts = ((0, 0, 128), (0, 128, 128), (1, 0, PAD), (2, 0, PAD), (3, 0, PAD))
+
+    def send_near(p):
+        n, w0, size = parts[p]
+        rows = pl.ds(w0, size)
+        remote(wst.at[kind_block(near, n), rows, :], wl.at[1, n, rows, :], wb_send, wb_recv.at[p], near_same).start()
+
     for n in range(4):
         remote(wst.at[kind_block(x, n)], wl.at[0, n], wp_send, wp_recv.at[n], partner).start()
 
@@ -142,35 +144,40 @@
             lax.fori_loop(0, 8, squares, 0)
     for d in range(1, 8):
         remote(ssq.at[row], ssq.at[row], ssq_send, ssq_recv.at[row], at_row(lax.rem(row + d, 8))).start()
-    for n in range(1, 4):
-        send_near(n)
 
     for f in range(4):
         rows = pl.ds(f * 512, 512)
         xst[rows, :] = h[pl.ds(pl.multiple_of(mate * HALF + f * 512, 512), 512), :].astype(F32)
         remote(xst.at[rows, :], xl.at[0, rows, :], xp_send, xp_recv.at[f], partner).start()
 
-    def relay_weights(n):
+    def relay_weights(p):
+        n, w0, size = parts[p]
+        rows = pl.ds(w0, size)
         with jax.named_scope("wrelay"):
-            drain_recv(wl.at[1, n], wb_recv.at[n])
-        remote(wl.at[1, n], wl.at[2, n], wr_send, wr_recv.at[n], partner).start()
-
-    def take_weights(n):
+            drain_recv(wl.at[1, n, rows, :], wb_recv.at[p])
+        remote(wl.at[1, n, rows, :], wl.at[2, n, rows, :], wr_send, wr_recv.at[p], partner).start()
+        if 1 <= p < 4:
+            send_near(p + 1)
+
+    def take_weights(p):
+        n, w0, size = parts[p]
+        rows = pl.ds(w0, size)
         with jax.named_scope("wtake"):
-            drain_recv(wl.at[0, n], wp_recv.at[n])
-            drain_recv(wl.at[2, n], wr_recv.at[n])
-        wbf[n, :, 0:512] = wst[kind_block(x, n)].astype(BF16)
+            if w0 == 0:
+                drain_recv(wl.at[0, n], wp_recv.at[n])
+            drain_recv(wl.at[2, n, rows, :], wr_recv.at[p])
+        wbf[n, rows, 0:512] = wst[kind_block(x, n), rows, :].astype(BF16)
         for k in range(3):
-            wbf[n, :, (k + 1) * 512:(k + 2) * 512] = wl[k, n].astype(BF16)
+            wbf[n, rows, (k + 1) * 512:(k + 2) * 512] = wl[k, n, rows, :].astype(BF16)
 
     ups = (at_col(lax.rem(y + 1, 4), z), at_col(lax.rem(y + 3, 4), z),
            at_col(y, lax.rem(z + 1, 4)), at_col(y, lax.rem(z + 3, 4)))
     along_first = (ups[0], ups[1], ups[2], ups[3])
     along_second = (ups[2], ups[3], ups[0], ups[1])
 
-    def serve(i, j):
+    def serve(i, j, flows=(0, 1, 2, 3)):
         with jax.named_scope("serve"):
-            for f in range(4):
+            for f in flows:
                 ref = xl.at[pl.ds(1, 2), piece_rows(f, i, j), :]
                 step = i * 4 + j
                 drain_recv(ref, x_recv.at[f, step])
@@ -206,43 +213,62 @@
                     raw, gain = xl[k - 1, rows, lanes], gl[k - 1, :, lanes]
                 xbf[rows, k * 512 + q * 128:k * 512 + (q + 1) * 128] = (raw * scale * gain).astype(BF16)
 
-    def share(left, n):
-        return lax.dot_general(left, wbf[n], (((1,), (1,)), ((), ())), preferred_element_type=F32)
-
-    def far_group(i, j):
+    def share(left, n, rows=slice(0, PAD)):
+        return lax.dot_general(left, wbf[n, rows, :], (((1,), (1,)), ((), ())), preferred_element_type=F32)
+
+    def far_group(i, j, words):
         with jax.named_scope("group"):
+            left = jnp.concatenate([xbf[piece_rows(f, i, j), :] for f in range(4)], axis=0)
+            value = share(left, 0, words)
+            lanes = pl.ds(words.start, words.stop - words.start)
+            for f in range(4):
+                rows = piece_rows(f, i, j)
+                zs[0, rows, words] = value[f * PIECE:(f + 1) * PIECE, :]
+                remote(zs.at[0, rows, lanes], zr.at[c, rows, lanes], z_send.at[0],
+                       z_recv.at[c, f * 4 + first(f, i)], at_row(far * 2)).start()
+
+    def normalise_group(i, j):
+        with jax.named_scope("norm"):
             for f in range(4):
                 normalise(f, i, j)
-            left = jnp.concatenate([xbf[piece_rows(f, i, j), :] for f in range(4)], axis=0)
-            value = share(left, 0)
-            for f in range(4):
-                rows = piece_rows(f, i, j)
-                zs[0, rows, :] = value[f * PIECE:(f + 1) * PIECE, :]
-                remote(zs.at[0, rows, :], zr.at[c, rows, :], z_send.at[0], z_recv.at[c, f * 4 + first(f, i)],
-                       at_row(far * 2)).start()
 
     order = sorted(((i, j) for i in range(4) for j in range(4)), key=lambda t: (t[0] + t[1], -t[0]))
-    ahead = AHEAD
-    for i, j in order[:ahead - 2]:
-        serve(i, j)
+    low, high, full = slice(0, 128), slice(128, PAD), slice(0, PAD)
+    serve(0, 0, (0, 1, 2))
+    drain_send(xl.at[0, pl.ds(0, 256), :], xb_send)
+    send_near(0)
+    send_near(1)
+    serve(0, 0, (3,))
+    serve(*order[1])
     scales()
-    serve(*order[ahead - 2])
-    relay_weights(0)
-    serve(*order[ahead - 1])
     for f in range(4):
         drain_recv(xl.at[0, pl.ds(f * 512, 512), :], xp_recv.at[f])
-    with jax.named_scope("take"):
-        take_weights(0)
-    for k, (i, j) in enumerate(order):
-        far_group(i, j)
-        if k > 0 and k + ahead - 1 < 16:
-            serve(*order[k + ahead - 1])
-        if k == 6:
+    serve(*order[2])
+    relay_weights(0)
+    normalise_group(*order[0])
+    normalise_group(*order[1])
+    take_weights(0)
+    far_group(*order[0], low)
+    far_group(*order[1], low)
+    for k in (2, 3):
+        normalise_group(*order[k])
+        far_group(*order[k], low)
+        serve(*order[k + 1])
+        if k == 2:
             relay_weights(1)
-        if k == 10:
+    take_weights(1)
+    for k in range(4):
+        far_group(*order[k], high)
+    for k in range(4, 16):
+        normalise_group(*order[k])
+        far_group(*order[k], full)
+        if k < 15:
+            serve(*order[k + 1])
+        if k == 8:
             relay_weights(2)
-    with jax.named_scope("take"):
-        take_weights(1)
+        if k == 12:
+            relay_weights(3)
+    take_weights(2)
 
     def block_rows(blk):
         return pl.ds(pl.multiple_of(blk * BLOCK, BLOCK), BLOCK)
@@ -255,9 +281,9 @@
         return 0
 
     lax.fori_loop(0, 16, step_far, 0)
-    relay_weights(3)
-    take_weights(2)
+    relay_weights(4)
     take_weights(3)
+    take_weights(4)
 
     def step_own(blk, _):
         with jax.named_scope("own"):
@@ -269,8 +295,7 @@
 
     lax.fori_loop(0, 16, step_own, 0)
 
-    def finish(p, half, q, mine):
-        blk = p * 4 + q
+    def finish(half, blk, mine):
         rows = block_rows(blk)
         with jax.named_scope("wz"):
             drain_recv(zr.at[half, rows, :], z_recv.at[half, blk])
@@ -284,47 +309,38 @@
         top = jnp.max(jnp.maximum(left, right).T, axis=0, keepdims=True)
         shift = jnp.broadcast_to(top, (BLOCK, BLOCK)).T
         mass = jnp.exp(left - shift) + jnp.exp(right - shift)
-        st1[p, row, 0, pl.ds(half * 4 + q, 1), :] = top
-        st1[p, row, 1, pl.ds(half * 4 + q, 1), :] = jnp.sum(mass.T, axis=0, keepdims=True)
-
-    def combine(st, p, count):
-        top = st[p, 0, 0]
-        for k in range(1, count):
-            top = jnp.maximum(top, st[p, k, 0])
-        mass = st[p, 0, 1] * jnp.exp(st[p, 0, 0] - top)
-        for k in range(1, count):
-            mass = mass + st[p, k, 1] * jnp.exp(st[p, k, 0] - top)
-        return top, mass
-
-    def exchange(st, p, me, count, send, recv, dev):
+        st[0, pl.ds(half * 16 + blk, 1), :] = top
+        st[1, pl.ds(half * 16 + blk, 1), :] = jnp.sum(mass.T, axis=0, keepdims=True)
+
+    def step_out(blk, _):
+        rows = block_rows(blk)
+        finish(c, blk, xl[0, rows, 0:256])
+        drain_recv(zp.at[rows, :], zp_recv.at[blk])
+        finish(mate, blk, zp[rows, :])
+        return 0
+
+    with jax.named_scope("finish"):
+        lax.fori_loop(0, 16, step_out, 0)
+
+    def exchange(buf, me, count, send, recv, dev):
         with jax.named_scope("exch"):
             for d in range(1, count):
-                remote(st.at[p, me], st.at[p, me], send, recv.at[p, me], dev(lax.rem(me + d, count))).start()
+                remote(buf.at[me], buf.at[me], send, recv.at[me], dev(lax.rem(me + d, count))).start()
             for d in range(1, count):
                 other = lax.rem(me + d, count)
-                drain_recv(st.at[p, other], recv.at[p, other])
-
-    for p in range(4):
-        def step_out(q, _, p=p):
-            rows = block_rows(p * 4 + q)
-            finish(p, c, q, xl[0, rows, 0:256])
-            drain_recv(zp.at[rows, :], zp_recv.at[p * 4 + q])
-            finish(p, mate, q, zp[rows, :])
-            return 0
-
-        with jax.named_scope("finish"):
-            lax.fori_loop(0, 4, step_out, 0)
-        exchange(st1, p, row, 8, st_send.at[0], st1_recv, at_row)
-        top, mass = combine(st1, p, 8)
-        st2[p, z, 0], st2[p, z, 1] = top, mass
-        exchange(st2, p, z, 4, st_send.at[1], st2_recv, lambda k: at_col(y, k))
-        top, mass = combine(st2, p, 4)
-        st3[p, y, 0], st3[p, y, 1] = top, mass
-        exchange(st3, p, y, 4, st_send.at[2], st3_recv, lambda k: at_col(k, z))
-        top, mass = combine(st3, p, 4)
-        lse = top + jnp.log(mass)
-        for half in range(2):
-            lse_ref[half * 16 + p * 4:half * 16 + p * 4 + 4, :] = lse[half * 4:half * 4 + 4, :]
+                drain_recv(buf.at[other], recv.at[other])
+        top = buf[0]
+        for k in range(1, count):
+            top = jnp.maximum(top, buf[k])
+        mass = jnp.exp(buf[0] - top)
+        for k in range(1, count):
+            mass = mass + jnp.exp(buf[k] - top)
+        return top + jnp.log(mass)
+
+    st1[row] = st[0] + jnp.log(st[1])
+    st2[z] = exchange(st1, row, 8, st_send.at[0], st1_recv, at_row)
+    st3[y] = exchange(st2, z, 4, st_send.at[1], st2_recv, lambda k: at_col(y, k))
+    lse_ref[...] = exchange(st3, y, 4, st_send.at[2], st3_recv, lambda k: at_col(k, z))
 
     drain_send(ssq.at[pl.ds(0, 7)], ssq_send)
     drain_send(gl, g_send)
@@ -332,15 +348,14 @@
     drain_send(wl.at[0], wb_send)
     drain_send(wl.at[0], wr_send)
     drain_send(xl.at[0], xp_send)
-    drain_send(xl.at[0, pl.ds(0, 256), :], xb_send)
     for f in range(4):
         drain_send(xl.at[pl.ds(1, 2), pl.ds(0, 15 * PIECE), :], xf_send.at[f])
     for n in range(2):
         drain_send(zs.at[n], z_send.at[n])
     drain_send(zp, zp_send)
-    drain_send(st1.at[:, pl.ds(0, 7)], st_send.at[0])
-    drain_send(st2.at[:, pl.ds(0, 3)], st_send.at[1])
-    drain_send(st3.at[:, pl.ds(0, 3)], st_send.at[2])
+    drain_send(st1.at[pl.ds(0, 7)], st_send.at[0])
+    drain_send(st2.at[pl.ds(0, 3)], st_send.at[1])
+    drain_send(st3.at[pl.ds(0, 3)], st_send.at[2])
     for half in range(2):
         pltpu.make_async_copy(zr.at[half], z_hbm.at[pl.ds(half * HALF, HALF), :], out_sem.at[half]).wait()
 
@@ -372,21 +387,22 @@
                 pltpu.VMEM((3, 1, FEAT), F32),
                 pltpu.VMEM((8, 32, 128), F32),
                 pltpu.VMEM((HALF, 128), F32),
-                pltpu.VMEM((4, 8, 2, 8, 128), F32),
-                pltpu.VMEM((4, 4, 2, 8, 128), F32),
-                pltpu.VMEM((4, 4, 2, 8, 128), F32),
+                pltpu.VMEM((2, 32, 128), F32),
+                pltpu.VMEM((8, 32, 128), F32),
+                pltpu.VMEM((4, 32, 128), F32),
+                pltpu.VMEM((4, 32, 128), F32),
                 dma((13,)),
                 dma, dma((8,)),
                 dma, dma((3,)),
                 dma, dma((4,)),
-                dma, dma((4,)),
-                dma, dma((4,)),
+                dma, dma((5,)),
+                dma, dma((5,)),
                 dma, dma((4,)),
                 dma, dma((4,)), dma((4, 16)),
                 dma((2,)), dma((2, 16)),
                 dma, dma((16,)),
                 dma((2,)),
-                dma((3,)), dma((4, 8)), dma((4, 4)), dma((4, 4)),
+                dma((3,)), dma((8,)), dma((4,)), dma((4,)),
             ],
             compiler_params=pltpu.CompilerParams(
                 collective_id=0, has_side_effects=True, vmem_limit_bytes=67_043_328),

time: 186 us -> 141 us (0.76)
  Pallas kernels: 181 us -> 136 us
    pallas_call x1, Pallas kernels: 181 us -> 136 us  [local_head(): pl.pallas_call(kernel, out_shape=(jax.ShapeDtypeStruct((SEQ, PAD), F32),...]
where the time goes in v4:
time: 141 us
  Pallas kernels  136 us (96%)
  other arithmetic  4.16 us (3%)
    pallas_call x1, Pallas kernels, local_head(): pl.pallas_call(kernel, out_shape=(jax.ShapeDtypeStruct((SEQ, PAD), F32),...  136 us
    sub x1, other arithmetic, local_head(): return (logits[:, :WORDS] - log_norm[:, None], log_norm)  4.16 us

profile of v4, /device:TPU:0, one launch (start us, length us, event | category | flops | bytes accessed | tf_op | source)
XLA Modules:
  0.0 140.9 jit_solution(14221391737136057810)
XLA Ops:
  0.6 135.5 %shard_map.50 = (f32[4096,256]{1,0:T(8,128)}, f32[32,128]{1,0:T(8,128)}) custom-call(bf16[4096,512]{1,0:T(8,128)(2,1)} %h_hbm.1, f32[1,512]{1,0:T(1,128)} %bitcast.6, bf16[2000,512]{1,0:T(8,128)(2,1)} %bitcast.3), custom_call_target="tpu_custom_call" | custom-call | tf_op jit(solution)/shard_map/pallas_call | solution.py:367
  136.2 0.0 copy-start
  136.2 4.2 %slice_subtract_fusion = f32[4096,250]{1,0:T(8,128)} fusion(f32[4096,256]{1,0:T(8,128)} %get-tuple-element.4, f32[4096]{0:T(1024)} %bitcast.4), kind=kLoop, calls=%fused_computation | loop fusion | flops 1024000 | bytes 8208384 | tf_op jit(solution)/shard_map/sub | solution.py:411
  140.3 0.0 copy-done
  140.3 0.6 copy.6
Async XLA Ops:
  136.2 4.2 %copy-start = (f32[32,128]{1,0:T(8,128)S(1)}, f32[32,128]{1,0:T(8,128)}, u32[]{:S(2)}) copy-start(f32[32,128]{1,0:T(8,128)} %get-tuple-element.5) | copy-start | bytes 49156

commit v5 on v4

--- a/solution.py
+++ b/solution.py
@@ -15,7 +15,7 @@
 
 SEQ, FEAT, WORDS, PAD = 4096, 512, 250, 256
 HALF = SEQ // 2
-BLOCK, PIECE = 128, 32
+BLOCK, PIECE, WAVE = 128, 32, 16
 
 
 def kernel(h_hbm, g_ref, w_hbm, z_hbm, lse_ref,
@@ -65,6 +65,10 @@
     def piece_rows(f, i, j, offset=0):
         return pl.ds(pl.multiple_of(offset + piece_base(f, i, j), PIECE), PIECE)
 
+    def wave_rows(f, t, offset=0):
+        v, i, j = t
+        return pl.ds(pl.multiple_of(offset + v * WAVE + piece_base(f, i, j), WAVE), WAVE)
+
     own_pieces = [(f, core) for f in range(4) for core in range(2)]
 
     def load_piece(f, core):
@@ -95,10 +99,13 @@
     with jax.named_scope("bar"):
         pl.semaphore_wait(barrier, len(peers))
 
-    for f, core in own_pieces:
-        slot = 1 + (core + c) - 2 * core * c
-        remote(hp.at[f * 2 + core], xl.at[slot, piece_rows(f, 0, 0), :], xb_send, x_recv.at[f, 0],
-               at_row(near * 2 + core)).start()
+    def send_pieces(v):
+        for f, core in own_pieces:
+            slot = 1 + (core + c) - 2 * core * c
+            remote(hp.at[f * 2 + core, pl.ds(v * WAVE, WAVE), :], xl.at[slot, wave_rows(f, (v, 0, 0)), :],
+                   xb_send.at[v], x_recv.at[f, v * 16], at_row(near * 2 + core)).start()
+
+    send_pieces(0)
     for slot, dev in enumerate((partner, near_same, near_other)):
         remote(g_ref, gl.at[slot], g_send, g_recv.at[slot], dev).start()
 
@@ -156,8 +163,6 @@
         with jax.named_scope("wrelay"):
             drain_recv(wl.at[1, n, rows, :], wb_recv.at[p])
         remote(wl.at[1, n, rows, :], wl.at[2, n, rows, :], wr_send, wr_recv.at[p], partner).start()
-        if 1 <= p < 4:
-            send_near(p + 1)
 
     def take_weights(p):
         n, w0, size = parts[p]
@@ -175,15 +180,36 @@
     along_first = (ups[0], ups[1], ups[2], ups[3])
     along_second = (ups[2], ups[3], ups[0], ups[1])
 
-    def serve(i, j, flows=(0, 1, 2, 3)):
+    def step_of(n):
+        i = 3 - lax.rem(n, 4)
+        reach = lax.div(n, 4) - i
+        return reach, (lax.div(reach, 4), i, lax.rem(reach, 4))
+
+    def each(lo, hi, body):
+        def at(n, _):
+            reach, t = step_of(n)
+
+            @pl.when((reach >= 0) & (reach < 8))
+            def _():
+                body(t)
+            return 0
+
+        lax.fori_loop(lo, hi, at, 0)
+
+    def serve(t, flows=(0, 1, 2, 3)):
+        v, i, j = t
         with jax.named_scope("serve"):
             for f in flows:
-                ref = xl.at[pl.ds(1, 2), piece_rows(f, i, j), :]
-                step = i * 4 + j
+                ref = xl.at[pl.ds(1, 2), wave_rows(f, t), :]
+                step = v * 16 + i * 4 + j
                 drain_recv(ref, x_recv.at[f, step])
-                if j == 0 and i < 3:
+
+                @pl.when((j == 0) & (i < 3))
+                def _():
                     remote(ref, ref, xf_send.at[f], x_recv.at[f, step + 4], along_first[f]).start()
-                if j < 3:
+
+                @pl.when(j < 3)
+                def _():
                     remote(ref, ref, xf_send.at[f], x_recv.at[f, step + 1], along_second[f]).start()
 
     def scales():
@@ -201,14 +227,14 @@
         for b in range(16):
             rcol[b * BLOCK:(b + 1) * BLOCK, :] = jnp.broadcast_to(inv[b:b + 1, :], (BLOCK, BLOCK)).T
 
-    def normalise(f, i, j):
-        rows = piece_rows(f, i, j)
+    def normalise(f, t):
+        rows = wave_rows(f, t)
         scale = rcol[rows, :]
         for k in range(4):
             for q in range(4):
                 lanes = slice(q * 128, (q + 1) * 128)
                 if k == 0:
-                    raw, gain = h[piece_rows(f, i, j, c * HALF), lanes].astype(F32), g_ref[:, lanes]
+                    raw, gain = h[wave_rows(f, t, c * HALF), lanes].astype(F32), g_ref[:, lanes]
                 else:
                     raw, gain = xl[k - 1, rows, lanes], gl[k - 1, :, lanes]
                 xbf[rows, k * 512 + q * 128:k * 512 + (q + 1) * 128] = (raw * scale * gain).astype(BF16)
@@ -216,58 +242,65 @@
     def share(left, n, rows=slice(0, PAD)):
         return lax.dot_general(left, wbf[n, rows, :], (((1,), (1,)), ((), ())), preferred_element_type=F32)
 
-    def far_group(i, j, words):
+    def far_group(t, words):
         with jax.named_scope("group"):
-            left = jnp.concatenate([xbf[piece_rows(f, i, j), :] for f in range(4)], axis=0)
+            left = jnp.concatenate([xbf[wave_rows(f, t), :] for f in range(4)], axis=0)
             value = share(left, 0, words)
             lanes = pl.ds(words.start, words.stop - words.start)
             for f in range(4):
-                rows = piece_rows(f, i, j)
-                zs[0, rows, words] = value[f * PIECE:(f + 1) * PIECE, :]
+                rows = wave_rows(f, t)
+                zs[0, rows, words] = value[f * WAVE:(f + 1) * WAVE, :]
                 remote(zs.at[0, rows, lanes], zr.at[c, rows, lanes], z_send.at[0],
-                       z_recv.at[c, f * 4 + first(f, i)], at_row(far * 2)).start()
-
-    def normalise_group(i, j):
+                       z_recv.at[c, f * 4 + first(f, t[1])], at_row(far * 2)).start()
+
+    def normalise_group(t):
         with jax.named_scope("norm"):
             for f in range(4):
-                normalise(f, i, j)
-
-    order = sorted(((i, j) for i in range(4) for j in range(4)), key=lambda t: (t[0] + t[1], -t[0]))
+                normalise(f, t)
+
     low, high, full = slice(0, 128), slice(128, PAD), slice(0, PAD)
-    serve(0, 0, (0, 1, 2))
-    drain_send(xl.at[0, pl.ds(0, 256), :], xb_send)
+    origin = tuple(jnp.int32(0) for _ in range(3))
+    serve(origin, (0, 1))
+    drain_send(xl.at[0, pl.ds(0, 128), :], xb_send.at[0])
     send_near(0)
     send_near(1)
-    serve(0, 0, (3,))
-    serve(*order[1])
+    serve(origin, (2, 3))
+    each(4, 8, serve)
     scales()
     for f in range(4):
         drain_recv(xl.at[0, pl.ds(f * 512, 512), :], xp_recv.at[f])
-    serve(*order[2])
     relay_weights(0)
-    normalise_group(*order[0])
-    normalise_group(*order[1])
+    each(0, 8, normalise_group)
+    each(8, 10, serve)
     take_weights(0)
-    far_group(*order[0], low)
-    far_group(*order[1], low)
-    for k in (2, 3):
-        normalise_group(*order[k])
-        far_group(*order[k], low)
-        serve(*order[k + 1])
-        if k == 2:
-            relay_weights(1)
+    each(0, 8, lambda t: far_group(t, low))
+
+    def low_step(t):
+        normalise_group(t)
+        far_group(t, low)
+
+    each(8, 10, low_step)
+    each(10, 12, lambda t: (serve(t), low_step(t)))
+    each(12, 14, lambda t: (serve(t), low_step(t)))
+    relay_weights(1)
+    send_pieces(1)
+    each(14, 16, lambda t: (serve(t), low_step(t)))
     take_weights(1)
-    for k in range(4):
-        far_group(*order[k], high)
-    for k in range(4, 16):
-        normalise_group(*order[k])
-        far_group(*order[k], full)
-        if k < 15:
-            serve(*order[k + 1])
-        if k == 8:
-            relay_weights(2)
-        if k == 12:
-            relay_weights(3)
+    each(0, 16, lambda t: far_group(t, high))
+
+    def full_step(t):
+        serve(t)
+        normalise_group(t)
+        far_group(t, full)
+
+    each(16, 20, full_step)
+    send_near(2)
+    each(20, 32, full_step)
+    relay_weights(2)
+    send_near(3)
+    each(32, 44, full_step)
+    relay_weights(3)
+    send_near(4)
     take_weights(2)
 
     def block_rows(blk):
@@ -348,6 +381,7 @@
     drain_send(wl.at[0], wb_send)
     drain_send(wl.at[0], wr_send)
     drain_send(xl.at[0], xp_send)
+    drain_send(xl.at[0, pl.ds(0, 128), :], xb_send.at[1])
     for f in range(4):
         drain_send(xl.at[pl.ds(1, 2), pl.ds(0, 15 * PIECE), :], xf_send.at[f])
     for n in range(2):
@@ -398,7 +432,7 @@
                 dma, dma((5,)),
                 dma, dma((5,)),
                 dma, dma((4,)),
-                dma, dma((4,)), dma((4, 16)),
+                dma((2,)), dma((4,)), dma((4, 32)),
                 dma((2,)), dma((2, 16)),
                 dma, dma((16,)),
                 dma((2,)),

time: 141 us -> 137 us (0.972)
  Pallas kernels: 136 us -> 132 us
    pallas_call x1, Pallas kernels: 136 us -> 132 us  [local_head(): pl.pallas_call(kernel, out_shape=(jax.ShapeDtypeStruct((SEQ, PAD), F32),...]
where the time goes in v5:
time: 137 us
  Pallas kernels  132 us (96%)
  other arithmetic  4.16 us (3%)
    pallas_call x1, Pallas kernels, local_head(): pl.pallas_call(kernel, out_shape=(jax.ShapeDtypeStruct((SEQ, PAD), F32),...  132 us
    sub x1, other arithmetic, local_head(): return (logits[:, :WORDS] - log_norm[:, None], log_norm)  4.16 us

profile of v5, /device:TPU:0, one launch (start us, length us, event | category | flops | bytes accessed | tf_op | source)
XLA Modules:
  0.0 137.0 jit_solution(16653678357614480354)
XLA Ops:
  0.6 131.5 %shard_map.50 = (f32[4096,256]{1,0:T(8,128)}, f32[32,128]{1,0:T(8,128)}) custom-call(bf16[4096,512]{1,0:T(8,128)(2,1)} %h_hbm.1, f32[1,512]{1,0:T(1,128)} %bitcast.6, bf16[2000,512]{1,0:T(8,128)(2,1)} %bitcast.3), custom_call_target="tpu_custom_call" | custom-call | tf_op jit(solution)/shard_map/pallas_call | solution.py:401
  132.2 0.0 copy-start
  132.2 4.2 %slice_subtract_fusion = f32[4096,250]{1,0:T(8,128)} fusion(f32[4096,256]{1,0:T(8,128)} %get-tuple-element.4, f32[4096]{0:T(1024)} %bitcast.4), kind=kLoop, calls=%fused_computation | loop fusion | flops 1024000 | bytes 8208384 | tf_op jit(solution)/shard_map/sub | solution.py:445
  136.4 0.0 copy-done
  136.4 0.6 copy.6
Async XLA Ops:
  132.2 4.2 %copy-start = (f32[32,128]{1,0:T(8,128)S(1)}, f32[32,128]{1,0:T(8,128)}, u32[]{:S(2)}) copy-start(f32[32,128]{1,0:T(8,128)} %get-tuple-element.5) | copy-start | bytes 49156

commit v6 on v5

--- a/solution.py
+++ b/solution.py
@@ -18,11 +18,11 @@
 BLOCK, PIECE, WAVE = 128, 32, 16
 
 
-def kernel(h_hbm, g_ref, w_hbm, z_hbm, lse_ref,
+def kernel(h_hbm, g_ref, w_hbm, z_ref, lse_ref,
            h, hp16, hp, w, wst, wl, wbf, xst, xl, xbf, zs, zp, zr, gl, ssq, rcol, st, st1, st2, st3,
            in_sem, ssq_send, ssq_recv, g_send, g_recv, wp_send, wp_recv, wb_send, wb_recv, wr_send, wr_recv,
            xp_send, xp_recv, xb_send, xf_send, x_recv, z_send, z_recv, zp_send, zp_recv,
-           out_sem, st_send, st1_recv, st2_recv, st3_recv):
+           st_send, st1_recv, st2_recv, st3_recv):
     col, row = lax.axis_index("col"), lax.axis_index("row")
     z, y = lax.div(col, 4), lax.rem(col, 4)
     x, c = lax.div(row, 2), lax.rem(row, 2)
@@ -281,26 +281,29 @@
 
     each(8, 10, low_step)
     each(10, 12, lambda t: (serve(t), low_step(t)))
-    each(12, 14, lambda t: (serve(t), low_step(t)))
     relay_weights(1)
     send_pieces(1)
-    each(14, 16, lambda t: (serve(t), low_step(t)))
+    for p in (2, 3, 4):
+        send_near(p)
+    each(12, 13, serve)
     take_weights(1)
-    each(0, 16, lambda t: far_group(t, high))
+    each(0, 12, lambda t: far_group(t, high))
 
     def full_step(t):
-        serve(t)
         normalise_group(t)
         far_group(t, full)
 
-    each(16, 20, full_step)
-    send_near(2)
-    each(20, 32, full_step)
+    each(12, 13, full_step)
+
+    def ring_step(t):
+        serve(t)
+        full_step(t)
+
+    each(13, 26, ring_step)
     relay_weights(2)
-    send_near(3)
-    each(32, 44, full_step)
+    each(26, 38, ring_step)
     relay_weights(3)
-    send_near(4)
+    each(38, 44, ring_step)
     take_weights(2)
 
     def block_rows(blk):
@@ -313,30 +316,31 @@
             remote(zs.at[1, rows, :], zr.at[c, rows, :], z_send.at[1], z_recv.at[c, blk], at_row(far * 2 + 1)).start()
         return 0
 
-    lax.fori_loop(0, 16, step_far, 0)
+    lax.fori_loop(0, 8, step_far, 0)
     relay_weights(4)
+    lax.fori_loop(8, 16, step_far, 0)
     take_weights(3)
     take_weights(4)
 
-    def step_own(blk, _):
+    def pair_rows(pair):
+        return pl.ds(pl.multiple_of(pair * 256, 256), 256)
+
+    def step_own(pair, _):
         with jax.named_scope("own"):
-            rows = block_rows(blk)
+            rows = pair_rows(pair)
             xl[0, rows, 256:512] = share(xbf[rows, :], 2 + mate)
-            remote(xl.at[0, rows, pl.ds(256, 256)], zp.at[rows, :], zp_send, zp_recv.at[blk], partner).start()
+            remote(xl.at[0, rows, pl.ds(256, 256)], zp.at[rows, :], zp_send, zp_recv.at[pair], partner).start()
             xl[0, rows, 0:256] = share(xbf[rows, :], 2 + c)
         return 0
 
-    lax.fori_loop(0, 16, step_own, 0)
+    lax.fori_loop(0, 8, step_own, 0)
 
     def finish(half, blk, mine):
         rows = block_rows(blk)
         with jax.named_scope("wz"):
             drain_recv(zr.at[half, rows, :], z_recv.at[half, blk])
         value = zr[half, rows, :] + mine
-        zr[half, rows, :] = value
-        pltpu.make_async_copy(
-            zr.at[half, rows, :],
-            z_hbm.at[pl.ds(pl.multiple_of(half * HALF + blk * BLOCK, BLOCK), BLOCK), :], out_sem.at[half]).start()
+        z_ref[pl.ds(pl.multiple_of(half * HALF + blk * BLOCK, BLOCK), BLOCK), :] = value
         lane = lax.broadcasted_iota(jnp.int32, (BLOCK, 128), 1)
         left, right = value[:, 0:128], jnp.where(lane < WORDS - 128, value[:, 128:256], LOW)
         top = jnp.max(jnp.maximum(left, right).T, axis=0, keepdims=True)
@@ -348,7 +352,12 @@
     def step_out(blk, _):
         rows = block_rows(blk)
         finish(c, blk, xl[0, rows, 0:256])
-        drain_recv(zp.at[rows, :], zp_recv.at[blk])
+
+        @pl.when(lax.rem(blk, 2) == 0)
+        def _():
+            pair = lax.div(blk, 2)
+            drain_recv(zp.at[pair_rows(pair), :], zp_recv.at[pair])
+
         finish(mate, blk, zp[rows, :])
         return 0
 
@@ -390,8 +399,6 @@
     drain_send(st1.at[pl.ds(0, 7)], st_send.at[0])
     drain_send(st2.at[pl.ds(0, 3)], st_send.at[1])
     drain_send(st3.at[pl.ds(0, 3)], st_send.at[2])
-    for half in range(2):
-        pltpu.make_async_copy(zr.at[half], z_hbm.at[pl.ds(half * HALF, HALF), :], out_sem.at[half]).wait()
 
 
 def solution(mesh):
@@ -400,10 +407,10 @@
     def local_head(hidden, norm_gain, w_head):
         logits, log_norm = pl.pallas_call(
             kernel,
-            out_shape=(jax.ShapeDtypeStruct((SEQ, PAD), F32), jax.ShapeDtypeStruct((32, 128), F32)),
+            out_shape=(pltpu.VMEM((SEQ, PAD), F32), jax.ShapeDtypeStruct((32, 128), F32)),
             in_specs=[pl.BlockSpec(memory_space=pl.ANY), pl.BlockSpec(memory_space=pltpu.VMEM),
                       pl.BlockSpec(memory_space=pl.ANY)],
-            out_specs=(pl.BlockSpec(memory_space=pl.ANY), pl.BlockSpec(memory_space=pltpu.VMEM)),
+            out_specs=(pl.BlockSpec(memory_space=pltpu.VMEM), pl.BlockSpec(memory_space=pltpu.VMEM)),
             scratch_shapes=[
                 pltpu.VMEM((SEQ, FEAT), BF16),
                 pltpu.VMEM((8, PIECE, FEAT), BF16),
@@ -434,12 +441,11 @@
                 dma, dma((4,)),
                 dma((2,)), dma((4,)), dma((4, 32)),
                 dma((2,)), dma((2, 16)),
-                dma, dma((16,)),
-                dma((2,)),
+                dma, dma((8,)),
                 dma((3,)), dma((8,)), dma((4,)), dma((4,)),
             ],
             compiler_params=pltpu.CompilerParams(
-                collective_id=0, has_side_effects=True, vmem_limit_bytes=67_043_328),
+                collective_id=0, has_side_effects=True, vmem_limit_bytes=59 * 1048576),
         )(hidden, norm_gain.reshape(1, FEAT), w_head.T)
         log_norm = log_norm.reshape(SEQ)
         return logits[:, :WORDS] - log_norm[:, None], log_norm

time: 137 us -> 136 us (level)
  no operation moved by 1% of the time
where the time goes in v6:
time: 136 us
  Pallas kernels  132 us (97%)
  other arithmetic  3.11 us (2%)
    pallas_call x1, Pallas kernels, local_head(): pl.pallas_call(kernel, out_shape=(pltpu.VMEM((SEQ, PAD), F32), jax.ShapeD...  132 us
    sub x1, other arithmetic, local_head(): return (logits[:, :WORDS] - log_norm[:, None], log_norm)  3.11 us

profile of v6, /device:TPU:0, one launch (start us, length us, event | category | flops | bytes accessed | tf_op | source)
XLA Modules:
  0.0 136.2 jit_solution(2035985193847595834)
XLA Ops:
  0.6 131.9 %shard_map.50 = (f32[4096,256]{1,0:T(8,128)S(1)}, f32[32,128]{1,0:T(8,128)}) custom-call(bf16[4096,512]{1,0:T(8,128)(2,1)} %h_hbm.1, f32[1,512]{1,0:T(1,128)} %bitcast.6, bf16[2000,512]{1,0:T(8,128)(2,1)} %bitcast.3), custom_call_target="tpu_custom_call" | custom-call | tf_op jit(solution)/shard_map/pallas_call | solution.py:408
  132.5 0.0 copy-start
  132.5 3.1 %slice_subtract_fusion = f32[4096,250]{1,0:T(8,128)} fusion(f32[4096,256]{1,0:T(8,128)S(1)} %get-tuple-element.4, f32[4096]{0:T(1024)} %bitcast.4), kind=kLoop, calls=%fused_computation | loop fusion | flops 1024000 | bytes 8208384 | tf_op jit(solution)/shard_map/sub | solution.py:451
  135.6 0.0 copy-done
  135.6 0.6 copy.6
Async XLA Ops:
  132.5 3.1 %copy-start = (f32[32,128]{1,0:T(8,128)S(1)}, f32[32,128]{1,0:T(8,128)}, u32[]{:S(2)}) copy-start(f32[32,128]{1,0:T(8,128)} %get-tuple-element.5) | copy-start | bytes 49156

commit v7 on v6

--- a/solution.py
+++ b/solution.py
@@ -15,13 +15,13 @@
 
 SEQ, FEAT, WORDS, PAD = 4096, 512, 250, 256
 HALF = SEQ // 2
-BLOCK, PIECE, WAVE = 128, 32, 16
+BLOCK, PIECE, WAVE, GROUP = 128, 32, 16, 64
 
 
 def kernel(h_hbm, g_ref, w_hbm, z_ref, lse_ref,
            h, hp16, hp, w, wst, wl, wbf, xst, xl, xbf, zs, zp, zr, gl, ssq, rcol, st, st1, st2, st3,
            in_sem, ssq_send, ssq_recv, g_send, g_recv, wp_send, wp_recv, wb_send, wb_recv, wr_send, wr_recv,
-           xp_send, xp_recv, xb_send, xf_send, x_recv, z_send, z_recv, zp_send, zp_recv,
+           xp_send, xp_recv, xb_send, xf_send, x_recv, z_send, z_recv, zq_recv, zp_send, zp_recv,
            st_send, st1_recv, st2_recv, st3_recv):
     col, row = lax.axis_index("col"), lax.axis_index("row")
     z, y = lax.div(col, 4), lax.rem(col, 4)
@@ -247,11 +247,10 @@
             left = jnp.concatenate([xbf[wave_rows(f, t), :] for f in range(4)], axis=0)
             value = share(left, 0, words)
             lanes = pl.ds(words.start, words.stop - words.start)
-            for f in range(4):
-                rows = wave_rows(f, t)
-                zs[0, rows, words] = value[f * WAVE:(f + 1) * WAVE, :]
-                remote(zs.at[0, rows, lanes], zr.at[c, rows, lanes], z_send.at[0],
-                       z_recv.at[c, f * 4 + first(f, t[1])], at_row(far * 2)).start()
+            rows = pl.ds(pl.multiple_of(((t[0] * 4 + t[1]) * 4 + t[2]) * GROUP, GROUP), GROUP)
+            zs[0, rows, words] = value
+            remote(zs.at[0, rows, lanes], zr.at[c, rows, lanes], z_send.at[0], zq_recv.at[c, t[1]],
+                   at_row(far * 2)).start()
 
     def normalise_group(t):
         with jax.named_scope("norm"):
@@ -335,11 +334,19 @@
 
     lax.fori_loop(0, 8, step_own, 0)
 
-    def finish(half, blk, mine):
-        rows = block_rows(blk)
-        with jax.named_scope("wz"):
-            drain_recv(zr.at[half, rows, :], z_recv.at[half, blk])
-        value = zr[half, rows, :] + mine
+    for pair in range(8):
+        drain_recv(zp.at[pair_rows(pair), :], zp_recv.at[pair])
+
+    def arrived(half, n, i, f, c2, s):
+        pieces = []
+        for b in range(4):
+            for v in range(2):
+                group = (v * 4 + i) * 4 + lax.rem(s * (c2 - b) + 4, 4)
+                start = c * (n * BLOCK + b * PIECE + v * WAVE) + mate * (group * GROUP + f * WAVE)
+                pieces.append(zr[half, pl.ds(pl.multiple_of(start, WAVE), WAVE), :])
+        return jnp.concatenate(pieces, axis=0)
+
+    def finish(half, blk, value):
         z_ref[pl.ds(pl.multiple_of(half * HALF + blk * BLOCK, BLOCK), BLOCK), :] = value
         lane = lax.broadcasted_iota(jnp.int32, (BLOCK, 128), 1)
         left, right = value[:, 0:128], jnp.where(lane < WORDS - 128, value[:, 128:256], LOW)
@@ -349,16 +356,24 @@
         st[0, pl.ds(half * 16 + blk, 1), :] = top
         st[1, pl.ds(half * 16 + blk, 1), :] = jnp.sum(mass.T, axis=0, keepdims=True)
 
-    def step_out(blk, _):
+    def step_out(n, _):
+        i, f = lax.div(n, 4), lax.rem(n, 4)
+        q, s = lax.div(f, 2), 1 - 2 * lax.rem(f, 2)
+        c1, c2 = y * (1 - q) + z * q, z * (1 - q) + y * q
+        blk = c * n + mate * (f * 4 + lax.rem(c1 - s * i + 4, 4))
+        with jax.named_scope("wz"):
+            @pl.when((c == 0) & (f == 0))
+            def _():
+                for half in range(2):
+                    drain_recv(zr.at[half, pl.ds(0, 512), :], zq_recv.at[half, i])
+
+            @pl.when(c == 1)
+            def _():
+                for half in range(2):
+                    drain_recv(zr.at[half, block_rows(n), :], z_recv.at[half, n])
         rows = block_rows(blk)
-        finish(c, blk, xl[0, rows, 0:256])
-
-        @pl.when(lax.rem(blk, 2) == 0)
-        def _():
-            pair = lax.div(blk, 2)
-            drain_recv(zp.at[pair_rows(pair), :], zp_recv.at[pair])
-
-        finish(mate, blk, zp[rows, :])
+        finish(c, blk, arrived(c, n, i, f, c2, s) + xl[0, rows, 0:256])
+        finish(mate, blk, arrived(mate, n, i, f, c2, s) + zp[rows, :])
         return 0
 
     with jax.named_scope("finish"):
@@ -407,7 +422,7 @@
     def local_head(hidden, norm_gain, w_head):
         logits, log_norm = pl.pallas_call(
             kernel,
-            out_shape=(pltpu.VMEM((SEQ, PAD), F32), jax.ShapeDtypeStruct((32, 128), F32)),
+            out_shape=(pltpu.VMEM((SEQ, PAD), F32), pltpu.VMEM((32, 128), F32)),
             in_specs=[pl.BlockSpec(memory_space=pl.ANY), pl.BlockSpec(memory_space=pltpu.VMEM),
                       pl.BlockSpec(memory_space=pl.ANY)],
             out_specs=(pl.BlockSpec(memory_space=pltpu.VMEM), pl.BlockSpec(memory_space=pltpu.VMEM)),
@@ -440,7 +455,7 @@
                 dma, dma((5,)),
                 dma, dma((4,)),
                 dma((2,)), dma((4,)), dma((4, 32)),
-                dma((2,)), dma((2, 16)),
+                dma((2,)), dma((2, 16)), dma((2, 4)),
                 dma, dma((8,)),
                 dma((3,)), dma((8,)), dma((4,)), dma((4,)),
             ],

time: 136 us -> 135 us (level)
  no operation moved by 1% of the time
where the time goes in v7:
time: 135 us
  Pallas kernels  131 us (97%)
  other arithmetic  2.37 us (2%)
    pallas_call x1, Pallas kernels, local_head(): pl.pallas_call(kernel, out_shape=(pltpu.VMEM((SEQ, PAD), F32), pltpu.VMEM...  131 us

profile of v7, /device:TPU:0, one launch (start us, length us, event | category | flops | bytes accessed | tf_op | source)
XLA Modules:
  0.0 134.7 jit_solution(16103310125858033390)
XLA Ops:
  0.6 131.1 %shard_map.50 = (f32[4096,256]{1,0:T(8,128)S(1)}, f32[32,128]{1,0:T(8,128)S(1)}) custom-call(bf16[4096,512]{1,0:T(8,128)(2,1)} %h_hbm.1, f32[1,512]{1,0:T(1,128)} %bitcast.6, bf16[2000,512]{1,0:T(8,128)(2,1)} %bitcast.5), custom_call_target="tpu_custom_call" | custom-call | tf_op jit(solution)/shard_map/pallas_call | solution.py:423
  131.7 2.4 %slice_subtract_fusion = f32[4096,250]{1,0:T(8,128)} fusion(f32[4096,256]{1,0:T(8,128)S(1)} %get-tuple-element.4, f32[4096]{0:T(1024)S(1)} %bitcast.3), kind=kLoop, calls=%fused_computation | loop fusion | flops 1024000 | bytes 8208384 | tf_op jit(solution)/shard_map/sub | solution.py:466
  134.1 0.6 copy.6

commit v8 on v7

--- a/solution.py
+++ b/solution.py
@@ -150,7 +150,9 @@
         with jax.named_scope("squares"):
             lax.fori_loop(0, 8, squares, 0)
     for d in range(1, 8):
-        remote(ssq.at[row], ssq.at[row], ssq_send, ssq_recv.at[row], at_row(lax.rem(row + d, 8))).start()
+        peer = lax.rem(row + d, 8)
+        theirs = ssq.at[row, pl.ds(pl.multiple_of(lax.rem(peer, 2) * 16, 16), 16), :]
+        remote(theirs, theirs, ssq_send, ssq_recv.at[row], at_row(peer)).start()
 
     for f in range(4):
         rows = pl.ds(f * 512, 512)
@@ -216,7 +218,7 @@
         with jax.named_scope("wssq"):
             for d in range(1, 8):
                 r = lax.rem(row + d, 8)
-                drain_recv(ssq.at[r], ssq_recv.at[r])
+                drain_recv(ssq.at[r, pl.ds(0, 16), :], ssq_recv.at[r])
             for slot in range(3):
                 drain_recv(gl.at[slot], g_recv.at[slot])
         mine = pl.ds(pl.multiple_of(c * 16, 16), 16)
@@ -259,11 +261,10 @@
 
     low, high, full = slice(0, 128), slice(128, PAD), slice(0, PAD)
     origin = tuple(jnp.int32(0) for _ in range(3))
-    serve(origin, (0, 1))
     drain_send(xl.at[0, pl.ds(0, 128), :], xb_send.at[0])
     send_near(0)
     send_near(1)
-    serve(origin, (2, 3))
+    serve(origin)
     each(4, 8, serve)
     scales()
     for f in range(4):
@@ -381,7 +382,7 @@
 
     def exchange(buf, me, count, send, recv, dev):
         with jax.named_scope("exch"):
-            for d in range(1, count):
+            for d in sorted(range(1, count), key=lambda d: abs(d - count // 2)):
                 remote(buf.at[me], buf.at[me], send, recv.at[me], dev(lax.rem(me + d, count))).start()
             for d in range(1, count):
                 other = lax.rem(me + d, count)
@@ -399,7 +400,7 @@
     st3[y] = exchange(st2, z, 4, st_send.at[1], st2_recv, lambda k: at_col(y, k))
     lse_ref[...] = exchange(st3, y, 4, st_send.at[2], st3_recv, lambda k: at_col(k, z))
 
-    drain_send(ssq.at[pl.ds(0, 7)], ssq_send)
+    drain_send(ssq.at[pl.ds(0, 7), pl.ds(0, 16), :], ssq_send)
     drain_send(gl, g_send)
     drain_send(wl.at[0], wp_send)
     drain_send(wl.at[0], wb_send)

time: 135 us -> 134 us (level)
  no operation moved by 1% of the time
where the time goes in v8:
time: 134 us; the launch traced here: 133 us
  Pallas kernels  130 us (97%)
  other arithmetic  2.37 us (2%)
    pallas_call x1, Pallas kernels, local_head(): pl.pallas_call(kernel, out_shape=(pltpu.VMEM((SEQ, PAD), F32), pltpu.VMEM...  130 us

profile of v8, /device:TPU:0, one launch (start us, length us, event | category | flops | bytes accessed | tf_op | source)
XLA Modules:
  0.0 133.5 jit_solution(11383856337257964297)
XLA Ops:
  0.6 129.9 %shard_map.50 = (f32[4096,256]{1,0:T(8,128)S(1)}, f32[32,128]{1,0:T(8,128)S(1)}) custom-call(bf16[4096,512]{1,0:T(8,128)(2,1)} %h_hbm.1, f32[1,512]{1,0:T(1,128)} %bitcast.6, bf16[2000,512]{1,0:T(8,128)(2,1)} %bitcast.5), custom_call_target="tpu_custom_call" | custom-call | tf_op jit(solution)/shard_map/pallas_call | solution.py:424
  130.5 2.4 %slice_subtract_fusion = f32[4096,250]{1,0:T(8,128)} fusion(f32[4096,256]{1,0:T(8,128)S(1)} %get-tuple-element.4, f32[4096]{0:T(1024)S(1)} %bitcast.3), kind=kLoop, calls=%fused_computation | loop fusion | flops 1024000 | bytes 8208384 | tf_op jit(solution)/shard_map/sub | solution.py:467
  132.9 0.6 copy.6

commit v9 on v8

--- a/solution.py
+++ b/solution.py
@@ -198,20 +198,21 @@
 
         lax.fori_loop(lo, hi, at, 0)
 
-    def serve(t, flows=(0, 1, 2, 3)):
+    def serve(t):
         v, i, j = t
+        step = v * 16 + i * 4 + j
         with jax.named_scope("serve"):
-            for f in flows:
-                ref = xl.at[pl.ds(1, 2), wave_rows(f, t), :]
-                step = v * 16 + i * 4 + j
+            refs = [xl.at[pl.ds(1, 2), wave_rows(f, t), :] for f in range(4)]
+            for f, ref in enumerate(refs):
                 drain_recv(ref, x_recv.at[f, step])
 
                 @pl.when((j == 0) & (i < 3))
                 def _():
                     remote(ref, ref, xf_send.at[f], x_recv.at[f, step + 4], along_first[f]).start()
 
-                @pl.when(j < 3)
-                def _():
+            @pl.when(j < 3)
+            def _():
+                for f, ref in enumerate(refs):
                     remote(ref, ref, xf_send.at[f], x_recv.at[f, step + 1], along_second[f]).start()
 
     def scales():
@@ -271,7 +272,6 @@
         drain_recv(xl.at[0, pl.ds(f * 512, 512), :], xp_recv.at[f])
     relay_weights(0)
     each(0, 8, normalise_group)
-    each(8, 10, serve)
     take_weights(0)
     each(0, 8, lambda t: far_group(t, low))
 
@@ -279,13 +279,12 @@
         normalise_group(t)
         far_group(t, low)
 
-    each(8, 10, low_step)
-    each(10, 12, lambda t: (serve(t), low_step(t)))
+    each(8, 11, lambda t: (serve(t), low_step(t)))
     relay_weights(1)
     send_pieces(1)
     for p in (2, 3, 4):
         send_near(p)
-    each(12, 13, serve)
+    each(11, 12, lambda t: (serve(t), low_step(t)))
     take_weights(1)
     each(0, 12, lambda t: far_group(t, high))
 
@@ -293,13 +292,11 @@
         normalise_group(t)
         far_group(t, full)
 
-    each(12, 13, full_step)
-
     def ring_step(t):
         serve(t)
         full_step(t)
 
-    each(13, 26, ring_step)
+    each(12, 26, ring_step)
     relay_weights(2)
     each(26, 38, ring_step)
     relay_weights(3)

time: 134 us -> 134 us (level)
  no operation moved by 1% of the time
where the time goes in v9:
time: 134 us; the launch traced here: 133 us
  Pallas kernels  130 us (97%)
  other arithmetic  2.37 us (2%)
    pallas_call x1, Pallas kernels, local_head(): pl.pallas_call(kernel, out_shape=(pltpu.VMEM((SEQ, PAD), F32), pltpu.VMEM...  130 us

profile of v9, /device:TPU:0, one launch (start us, length us, event | category | flops | bytes accessed | tf_op | source)
XLA Modules:
  0.0 133.4 jit_solution(3889350124286937253)
XLA Ops:
  0.6 129.8 %shard_map.50 = (f32[4096,256]{1,0:T(8,128)S(1)}, f32[32,128]{1,0:T(8,128)S(1)}) custom-call(bf16[4096,512]{1,0:T(8,128)(2,1)} %h_hbm.1, f32[1,512]{1,0:T(1,128)} %bitcast.6, bf16[2000,512]{1,0:T(8,128)(2,1)} %bitcast.5), custom_call_target="tpu_custom_call" | custom-call | tf_op jit(solution)/shard_map/pallas_call | solution.py:421
  130.5 2.4 %slice_subtract_fusion = f32[4096,250]{1,0:T(8,128)} fusion(f32[4096,256]{1,0:T(8,128)S(1)} %get-tuple-element.4, f32[4096]{0:T(1024)S(1)} %bitcast.3), kind=kLoop, calls=%fused_computation | loop fusion | flops 1024000 | bytes 8208384 | tf_op jit(solution)/shard_map/sub | solution.py:464
  132.8 0.6 copy.6

commit v10 on v9

--- a/solution.py
+++ b/solution.py
@@ -260,6 +260,23 @@
             for f in range(4):
                 normalise(f, t)
 
+    def block_rows(blk):
+        return pl.ds(pl.multiple_of(blk * BLOCK, BLOCK), BLOCK)
+
+    def block_of(n):
+        i, f = lax.div(n, 4), lax.rem(n, 4)
+        q, s = lax.div(f, 2), 1 - 2 * lax.rem(f, 2)
+        c1, c2 = y * (1 - q) + z * q, z * (1 - q) + y * q
+        return i, f, f * 4 + lax.rem(c1 - s * i + 4, 4), c2, s
+
+    def step_far(n, _):
+        with jax.named_scope("far"):
+            blk = block_of(n)[2]
+            rows = block_rows(blk)
+            zs[1, rows, :] = share(xbf[rows, :], 1)
+            remote(zs.at[1, rows, :], zr.at[c, rows, :], z_send.at[1], z_recv.at[c, blk], at_row(far * 2 + 1)).start()
+        return 0
+
     low, high, full = slice(0, 128), slice(128, PAD), slice(0, PAD)
     origin = tuple(jnp.int32(0) for _ in range(3))
     drain_send(xl.at[0, pl.ds(0, 128), :], xb_send.at[0])
@@ -298,24 +315,21 @@
 
     each(12, 26, ring_step)
     relay_weights(2)
-    each(26, 38, ring_step)
+    each(26, 32, ring_step)
+    take_weights(2)
+
+    def mixed_step(n, _):
+        each(n, n + 1, ring_step)
+        return step_far(n - 32, 0)
+
+    lax.fori_loop(32, 36, mixed_step, 0)
+    each(36, 38, ring_step)
     relay_weights(3)
     each(38, 44, ring_step)
-    take_weights(2)
-
-    def block_rows(blk):
-        return pl.ds(pl.multiple_of(blk * BLOCK, BLOCK), BLOCK)
-
-    def step_far(blk, _):
-        with jax.named_scope("far"):
-            rows = block_rows(blk)
-            zs[1, rows, :] = share(xbf[rows, :], 1)
-            remote(zs.at[1, rows, :], zr.at[c, rows, :], z_send.at[1], z_recv.at[c, blk], at_row(far * 2 + 1)).start()
-        return 0
-
-    lax.fori_loop(0, 8, step_far, 0)
+
+    lax.fori_loop(4, 10, step_far, 0)
     relay_weights(4)
-    lax.fori_loop(8, 16, step_far, 0)
+    lax.fori_loop(10, 16, step_far, 0)
     take_weights(3)
     take_weights(4)
 
@@ -335,12 +349,12 @@
     for pair in range(8):
         drain_recv(zp.at[pair_rows(pair), :], zp_recv.at[pair])
 
-    def arrived(half, n, i, f, c2, s):
+    def arrived(half, i, f, blk, c2, s):
         pieces = []
         for b in range(4):
             for v in range(2):
                 group = (v * 4 + i) * 4 + lax.rem(s * (c2 - b) + 4, 4)
-                start = c * (n * BLOCK + b * PIECE + v * WAVE) + mate * (group * GROUP + f * WAVE)
+                start = c * (blk * BLOCK + b * PIECE + v * WAVE) + mate * (group * GROUP + f * WAVE)
                 pieces.append(zr[half, pl.ds(pl.multiple_of(start, WAVE), WAVE), :])
         return jnp.concatenate(pieces, axis=0)
 
@@ -355,10 +369,7 @@
         st[1, pl.ds(half * 16 + blk, 1), :] = jnp.sum(mass.T, axis=0, keepdims=True)
 
     def step_out(n, _):
-        i, f = lax.div(n, 4), lax.rem(n, 4)
-        q, s = lax.div(f, 2), 1 - 2 * lax.rem(f, 2)
-        c1, c2 = y * (1 - q) + z * q, z * (1 - q) + y * q
-        blk = c * n + mate * (f * 4 + lax.rem(c1 - s * i + 4, 4))
+        i, f, blk, c2, s = block_of(n)
         with jax.named_scope("wz"):
             @pl.when((c == 0) & (f == 0))
             def _():
@@ -368,11 +379,22 @@
             @pl.when(c == 1)
             def _():
                 for half in range(2):
-                    drain_recv(zr.at[half, block_rows(n), :], z_recv.at[half, n])
+                    drain_recv(zr.at[half, block_rows(blk), :], z_recv.at[half, blk])
         rows = block_rows(blk)
-        finish(c, blk, arrived(c, n, i, f, c2, s) + xl[0, rows, 0:256])
-        finish(mate, blk, arrived(mate, n, i, f, c2, s) + zp[rows, :])
+        finish(c, blk, arrived(c, i, f, blk, c2, s) + xl[0, rows, 0:256])
+        finish(mate, blk, arrived(mate, i, f, blk, c2, s) + zp[rows, :])
         return 0
+
+    drain_send(ssq.at[pl.ds(0, 7), pl.ds(0, 16), :], ssq_send)
+    drain_send(gl, g_send)
+    drain_send(wl.at[0], wp_send)
+    drain_send(wl.at[0], wb_send)
+    drain_send(wl.at[0], wr_send)
+    drain_send(xl.at[0], xp_send)
+    drain_send(xl.at[0, pl.ds(0, 128), :], xb_send.at[1])
+    for f in range(4):
+        drain_send(xl.at[pl.ds(1, 2), pl.ds(0, 15 * PIECE), :], xf_send.at[f])
+    drain_send(zp, zp_send)
 
     with jax.named_scope("finish"):
         lax.fori_loop(0, 16, step_out, 0)
@@ -394,21 +416,11 @@
 
     st1[row] = st[0] + jnp.log(st[1])
     st2[z] = exchange(st1, row, 8, st_send.at[0], st1_recv, at_row)
+    for n in range(2):
+        drain_send(zs.at[n], z_send.at[n])
     st3[y] = exchange(st2, z, 4, st_send.at[1], st2_recv, lambda k: at_col(y, k))
     lse_ref[...] = exchange(st3, y, 4, st_send.at[2], st3_recv, lambda k: at_col(k, z))
 
-    drain_send(ssq.at[pl.ds(0, 7), pl.ds(0, 16), :], ssq_send)
-    drain_send(gl, g_send)
-    drain_send(wl.at[0], wp_send)
-    drain_send(wl.at[0], wb_send)
-    drain_send(wl.at[0], wr_send)
-    drain_send(xl.at[0], xp_send)
-    drain_send(xl.at[0, pl.ds(0, 128), :], xb_send.at[1])
-    for f in range(4):
-        drain_send(xl.at[pl.ds(1, 2), pl.ds(0, 15 * PIECE), :], xf_send.at[f])
-    for n in range(2):
-        drain_send(zs.at[n], z_send.at[n])
-    drain_send(zp, zp_send)
     drain_send(st1.at[pl.ds(0, 7)], st_send.at[0])
     drain_send(st2.at[pl.ds(0, 3)], st_send.at[1])
     drain_send(st3.at[pl.ds(0, 3)], st_send.at[2])

time: 134 us -> 134 us (level)
  no operation moved by 1% of the time
where the time goes in v10:
time: 134 us; the launch traced here: 133 us
  Pallas kernels  130 us (97%)
  other arithmetic  2.37 us (2%)
    pallas_call x1, Pallas kernels, local_head(): pl.pallas_call(kernel, out_shape=(pltpu.VMEM((SEQ, PAD), F32), pltpu.VMEM...  130 us

profile of v10, /device:TPU:0, one launch (start us, length us, event | category | flops | bytes accessed | tf_op | source)
XLA Modules:
  0.0 133.4 jit_solution(18008210552163253518)
XLA Ops:
  0.6 129.8 %shard_map.50 = (f32[4096,256]{1,0:T(8,128)S(1)}, f32[32,128]{1,0:T(8,128)S(1)}) custom-call(bf16[4096,512]{1,0:T(8,128)(2,1)} %h_hbm.1, f32[1,512]{1,0:T(1,128)} %bitcast.6, bf16[2000,512]{1,0:T(8,128)(2,1)} %bitcast.5), custom_call_target="tpu_custom_call" | custom-call | tf_op jit(solution)/shard_map/pallas_call | solution.py:433
  130.4 2.4 %slice_subtract_fusion = f32[4096,250]{1,0:T(8,128)} fusion(f32[4096,256]{1,0:T(8,128)S(1)} %get-tuple-element.4, f32[4096]{0:T(1024)S(1)} %bitcast.3), kind=kLoop, calls=%fused_computation | loop fusion | flops 1024000 | bytes 8208384 | tf_op jit(solution)/shard_map/sub | solution.py:476
  132.8 0.6 copy.6

commit v11 on v10

--- a/solution.py
+++ b/solution.py
@@ -133,8 +133,10 @@
         rows = pl.ds(w0, size)
         remote(wst.at[kind_block(near, n), rows, :], wl.at[1, n, rows, :], wb_send, wb_recv.at[p], near_same).start()
 
-    for n in range(4):
+    def send_partner(n):
         remote(wst.at[kind_block(x, n)], wl.at[0, n], wp_send, wp_recv.at[n], partner).start()
+
+    send_partner(0)
 
     for k in range(4):
         load_h(k).wait()
@@ -301,6 +303,8 @@
     send_pieces(1)
     for p in (2, 3, 4):
         send_near(p)
+    for n in range(1, 4):
+        send_partner(n)
     each(11, 12, lambda t: (serve(t), low_step(t)))
     take_weights(1)
     each(0, 12, lambda t: far_group(t, high))
@@ -415,11 +419,11 @@
         return top + jnp.log(mass)
 
     st1[row] = st[0] + jnp.log(st[1])
-    st2[z] = exchange(st1, row, 8, st_send.at[0], st1_recv, at_row)
+    st3[y] = exchange(st1, row, 8, st_send.at[0], st1_recv, at_row)
     for n in range(2):
         drain_send(zs.at[n], z_send.at[n])
-    st3[y] = exchange(st2, z, 4, st_send.at[1], st2_recv, lambda k: at_col(y, k))
-    lse_ref[...] = exchange(st3, y, 4, st_send.at[2], st3_recv, lambda k: at_col(k, z))
+    st2[z] = exchange(st3, y, 4, st_send.at[2], st3_recv, lambda k: at_col(k, z))
+    lse_ref[...] = exchange(st2, z, 4, st_send.at[1], st2_recv, lambda k: at_col(y, k))
 
     drain_send(st1.at[pl.ds(0, 7)], st_send.at[0])
     drain_send(st2.at[pl.ds(0, 3)], st_send.at[1])

time: 134 us -> 134 us (level)
  no operation moved by 1% of the time
where the time goes in v11:
time: 134 us; the launch traced here: 133 us
  Pallas kernels  130 us (97%)
  other arithmetic  2.37 us (2%)
    pallas_call x1, Pallas kernels, local_head(): pl.pallas_call(kernel, out_shape=(pltpu.VMEM((SEQ, PAD), F32), pltpu.VMEM...  130 us

profile of v11, /device:TPU:0, one launch (start us, length us, event | category | flops | bytes accessed | tf_op | source)
XLA Modules:
  0.0 133.4 jit_solution(12582724064546581195)
XLA Ops:
  0.6 129.8 %shard_map.50 = (f32[4096,256]{1,0:T(8,128)S(1)}, f32[32,128]{1,0:T(8,128)S(1)}) custom-call(bf16[4096,512]{1,0:T(8,128)(2,1)} %h_hbm.1, f32[1,512]{1,0:T(1,128)} %bitcast.6, bf16[2000,512]{1,0:T(8,128)(2,1)} %bitcast.5), custom_call_target="tpu_custom_call" | custom-call | tf_op jit(solution)/shard_map/pallas_call | solution.py:437
  130.4 2.4 %slice_subtract_fusion = f32[4096,250]{1,0:T(8,128)} fusion(f32[4096,256]{1,0:T(8,128)S(1)} %get-tuple-element.4, f32[4096]{0:T(1024)S(1)} %bitcast.3), kind=kLoop, calls=%fused_computation | loop fusion | flops 1024000 | bytes 8208384 | tf_op jit(solution)/shard_map/sub | solution.py:480
  132.8 0.6 copy.6
